TPU v7x, 128 devices: a whole 4x4x4 slice. The times are simulated.
128 devices in a mesh: dp: 128 (over z, y, x, core).
Axes of the slice: x: 4, y: 4, z: 4, core: 2. Of those that a mesh axis runs over, the one named last changes fastest.
Arguments:
- user_x: float32 [16384, 256], P('dp')
- item_x: float32 [16384, 256], P('dp')
- item_id: int32 [16384], P('dp')
- log_q: float32 [16384], P('dp')
- user_w1: float32 [256, 384], replicated
- user_w2: float32 [384, 384], replicated
- user_w3: float32 [384, 128], replicated
- item_w1: float32 [256, 384], replicated
- item_w2: float32 [384, 384], replicated
- item_w3: float32 [384, 128], replicated
Outputs:
- output 1: float32 [], replicated
- output 2: float32 [256, 384], replicated
- output 3: float32 [384, 384], replicated
- output 4: float32 [384, 128], replicated
- output 5: float32 [256, 384], replicated
- output 6: float32 [384, 384], replicated
- output 7: float32 [384, 128], replicated
All inputs are finite; a program needn't handle non-finite values.
Results may differ from a plain program's by a relative error of at most 0.0021784.
Values are sent between devices in bfloat16 or wider.
A program may use at most 1 GiB of HBM per device.

v0:
```python
import jax
import jax.numpy as jnp
from jax import lax
from jax.sharding import PartitionSpec as P

value_a11 = 0.05
INV_TEMP = 1.0 / value_a11
NORM_EPS = 1e-6
ROW_DIMS = (((0,), (0,)), ((), ()))
COL_DIMS = (((1,), (1,)), ((), ()))


def tower_forward(inputs, w_one, w_two, w_three):
    x_half = inputs.astype(jnp.bfloat16)
    pre_one = jnp.dot(x_half, w_one, preferred_element_type=jnp.float32)
    act_one = jnp.maximum(pre_one, 0.0).astype(jnp.bfloat16)
    pre_two = jnp.dot(act_one, w_two, preferred_element_type=jnp.float32)
    act_two = jnp.maximum(pre_two, 0.0).astype(jnp.bfloat16)
    raw_out = jnp.dot(act_two, w_three, preferred_element_type=jnp.float32)
    inv_norm = lax.rsqrt(jnp.sum(raw_out * raw_out, axis=1, keepdims=True) + NORM_EPS)
    return (x_half, pre_one, act_one, pre_two, act_two, raw_out * inv_norm, inv_norm)


def tower_backward(saved, w_two, w_three, grad_unit):
    x_half, pre_one, act_one, pre_two, act_two, unit_out, inv_norm = saved
    grad_raw = inv_norm * (grad_unit - unit_out * jnp.sum(unit_out * grad_unit, axis=1, keepdims=True))
    grad_raw_h = grad_raw.astype(jnp.bfloat16)
    grad_three = lax.dot_general(act_two, grad_raw_h, ROW_DIMS, preferred_element_type=jnp.float32)
    grad_act_two = lax.dot_general(grad_raw_h, w_three, COL_DIMS, preferred_element_type=jnp.float32)
    grad_pre_two = jnp.where(pre_two > 0.0, grad_act_two, 0.0).astype(jnp.bfloat16)
    grad_two = lax.dot_general(act_one, grad_pre_two, ROW_DIMS, preferred_element_type=jnp.float32)
    grad_act_one = lax.dot_general(grad_pre_two, w_two, COL_DIMS, preferred_element_type=jnp.float32)
    grad_pre_one = jnp.where(pre_one > 0.0, grad_act_one, 0.0).astype(jnp.bfloat16)
    grad_one = lax.dot_general(x_half, grad_pre_one, ROW_DIMS, preferred_element_type=jnp.float32)
    return (grad_one, grad_two, grad_three)


def solution(mesh):
    def device_step(user_x, item_x, item_id, log_q, user_w1, user_w2, user_w3, item_w1, item_w2, item_w3):
        user_ws = (user_w1.astype(jnp.bfloat16), user_w2.astype(jnp.bfloat16), user_w3.astype(jnp.bfloat16))
        item_ws = (item_w1.astype(jnp.bfloat16), item_w2.astype(jnp.bfloat16), item_w3.astype(jnp.bfloat16))
        user_saved = tower_forward(user_x, user_ws[0], user_ws[1], user_ws[2])
        item_saved = tower_forward(item_x, item_ws[0], item_ws[1], item_ws[2])
        user_half = user_saved[5].astype(jnp.bfloat16)
        item_half = item_saved[5].astype(jnp.bfloat16)
        item_all = lax.all_gather(item_half, 'dp', axis=0, tiled=True)
        logq_all = lax.all_gather(log_q, 'dp', axis=0, tiled=True)
        id_all = lax.all_gather(item_id, 'dp', axis=0, tiled=True)
        local_rows = user_x.shape[0]
        batch = item_all.shape[0]
        query_pos = lax.axis_index('dp') * local_rows + jnp.arange(local_rows)
        cand_pos = jnp.arange(batch)
        is_self = query_pos[:, None] == cand_pos[None, :]
        dropped = jnp.logical_and(item_id[:, None] == id_all[None, :], jnp.logical_not(is_self))
        raw = lax.dot_general(user_half, item_all, COL_DIMS, preferred_element_type=jnp.float32) * INV_TEMP - logq_all[None, :]
        scores = jnp.where(dropped, -jnp.inf, raw)
        row_max = jnp.max(scores, axis=1, keepdims=True)
        exp_scores = jnp.exp(scores - row_max)
        row_total = jnp.sum(exp_scores, axis=1, keepdims=True)
        log_norm = row_max[:, 0] + jnp.log(row_total[:, 0])
        pos_score = jnp.sum(user_half.astype(jnp.float32) * item_half.astype(jnp.float32), axis=1) * INV_TEMP - log_q
        softmax_rows = exp_scores / row_total
        grad_scores = (jnp.where(is_self, softmax_rows - 1.0, softmax_rows) / batch).astype(jnp.bfloat16)
        grad_user = jnp.dot(grad_scores, item_all, preferred_element_type=jnp.float32) * INV_TEMP
        item_part = lax.dot_general(grad_scores, user_half, ROW_DIMS, preferred_element_type=jnp.float32) * INV_TEMP
        grad_item = lax.psum_scatter(item_part, 'dp', scatter_dimension=0, tiled=True)
        user_grads = tower_backward(user_saved, user_ws[1], user_ws[2], grad_user)
        item_grads = tower_backward(item_saved, item_ws[1], item_ws[2], grad_item)
        totals = lax.psum((jnp.sum(log_norm - pos_score),) + user_grads + item_grads, 'dp')
        return (totals[0] / batch,) + tuple(totals[1:])

    batch_spec = P('dp', None)
    vec_spec = P('dp')
    whole = P()
    return jax.shard_map(device_step, mesh=mesh,
                         in_specs=(batch_spec, batch_spec, vec_spec, vec_spec, whole, whole, whole, whole, whole, whole),
                         out_specs=(whole, whole, whole, whole, whole, whole, whole), check_vma=False)
```

profile of v0, /device:TPU:1, one launch (start us, length us, event | category | flops | bytes accessed | tf_op | source)
XLA Modules:
  0.0 932.8 jit_solution(7470636075015810656)
XLA Ops:
  7.2 0.0 all-gather.4.cloned.1.call-start
  7.2 1.3 fusion.13
  8.5 1.3 fusion.23
  9.8 1.2 multiply_reduce_fusion.4
  10.9 1.3 fusion.11
  12.2 1.3 fusion.19
  13.5 1.2 multiply_reduce_fusion.3
  14.6 0.6 multiply_reduce_fusion.2
  15.3 0.0 all-gather.4.cloned.1.call-update
  15.3 0.0 reduce-scatter.2.cloned.1.call-start
  15.4 38.8 %all-gather.1 = f32[128,1,128]{2,1,0:T(1,128)S(1)} all-gather(f32[1,1,128]{2,1,0:T(1,128)} %bitcast.24), channel_id=1, replica_groups=mesh['dp'=128] {'dp'}, dimensions={0}, use_global_device_ids=true | all-gather | bytes 66048 | tf_op jit(solution)/shard_map/all_gather | solution.py:47
  54.2 33.3 %all-gather = s32[128,1,128]{2,1,0:T(1,128)S(1)} all-gather(s32[1,1,128]{2,1,0:T(1,128)} %bitcast.25), channel_id=1, replica_groups=mesh['dp'=128] {'dp'}, dimensions={0}, use_global_device_ids=true | all-gather | bytes 66048 | tf_op jit(solution)/shard_map/all_gather | solution.py:48
  87.5 0.0 all-gather.4.cloned.1.call-done
  87.5 5.8 fusion.51
  93.3 1.6 fusion.6
  94.9 2.6 fusion.3
  97.4 0.0 copy-start
  97.4 1.9 copy-done
  99.4 4.5 convolution_multiply_fusion
  103.9 0.0 copy-start.3
  103.9 0.0 copy-start.1
  103.9 0.0 copy-start.5
  103.9 0.0 copy-start.4
  103.9 0.0 reduce-scatter.2.cloned.1.call-update
  103.9 0.0 copy-start.2
  103.9 0.0 copy-start.6
  103.9 0.0 copy-start.7
  103.9 0.0 all-reduce.3.cloned.1.call-start
  104.0 4.8 multiply_reduce_fusion.1
  108.8 0.9 fusion.34
  109.7 0.0 copy-done.3
  109.7 0.2 fusion.7
  109.9 1.1 fusion.33
  111.0 0.0 copy-done.1
  111.0 0.0 copy-done.5
  111.0 1.2 convolution_bitcast_fusion.1
  112.3 640.7 %reduce-scatter.2.cloned.1.call-done = f32[128,128]{0,1:T(8,128)} async-done(((f32[16384,128]{0,1:T(8,128)}), f32[128,128]{0,1:T(8,128)}) %reduce-scatter.2.cloned.1.call-update) | async-done | bytes 65552 | tf_op jit(solution)/shard_map/reduce_scatter | solution.py:66
  752.9 0.9 multiply_reduce_fusion
  753.8 0.9 multiply_convert_fusion
  754.7 0.0 copy-done.4
  754.7 0.2 fusion.9
  754.9 0.9 fusion.36
  755.8 0.0 copy-done.2
  755.8 0.0 copy-done.6
  755.8 1.2 convolution_bitcast_fusion
  757.0 1.1 fusion.35
  758.1 0.0 all-reduce.3.cloned.1.call-update
  758.1 0.0 copy-done.7
  758.1 0.6 subtract_reduce_fusion
  758.7 69.7 %psum.49 = f32[]{:T(128)} all-reduce(f32[]{:T(128)} %subtract_reduce_fusion), channel_id=1, replica_groups=mesh['dp'=128] {'dp'}, use_global_device_ids=true, to_apply=%region_6.7 | all-reduce | flops 1 | bytes 8 | tf_op jit(solution)/shard_map/psum | solution.py:69
  829.1 85.1 %all-reduce.3.cloned.1.call-done = (f32[256,384]{0,1:T(8,128)}, f32[384,384]{1,0:T(8,128)}, f32[384,128]{1,0:T(8,128)}, f32[256,384]{0,1:T(8,128)}, f32[384,384]{1,0:T(8,128)}, /*index=5*/f32[384,128]{1,0:T(8,128)}) async-done(((f32[256,384]{0,1:T(8,128)}, f32[384,384]{1,0:T(8,128)}, f32[384,128]{1,0:T(8,128)}, f32[256,384]{0,1:T(8,128)}, f32[384,384]{1,0:T(8,128)}, /*index=5*/f32[384,128]{1,0:T(8,128)}), ...) | async-done | bytes 2359312 | tf_op jit(solution)/shard_map/psum | solution.py:69
  914.2 1.9 copy.21
  916.2 1.9 copy.22
  918.1 1.9 copy.30
  920.0 1.6 copy.31
  921.6 1.9 copy.32
  923.5 1.6 copy.33
  (3 shorter events, 0.0 us)
Async XLA Ops:
  7.2 80.3 %all-gather.4.cloned.1.call-start = ((), (), s32[]{:S(2)}) async-start(), calls=%async_computation.1 | async-start | bytes 4227072 | tf_op jit(solution)/shard_map/all_gather | solution.py:46
  15.3 737.6 %reduce-scatter.2.cloned.1.call-start = ((), (), s32[]{:S(2)}) async-start(), calls=%async_computation.2 | async-start | bytes 8454144 | tf_op jit(solution)/shard_map/reduce_scatter | solution.py:66
  97.4 2.0 copy-start
  103.9 5.9 copy-start.3
  103.9 7.2 copy-start.1
  103.9 7.2 copy-start.5
  103.9 650.8 %copy-start.4 = (f32[384,128]{1,0:T(8,128)S(1)}, f32[384,128]{1,0:T(8,128)}, u32[]{:S(2)}) copy-start(f32[384,128]{1,0:T(8,128)} %param.19) | copy-start | bytes 589828
  103.9 651.9 %copy-start.2 = (f32[384,384]{1,0:T(8,128)S(1)}, f32[384,384]{1,0:T(8,128)}, u32[]{:S(2)}) copy-start(f32[384,384]{1,0:T(8,128)} %param.18) | copy-start | bytes 1769476
  103.9 651.9 %copy-start.6 = (f32[128,256]{1,0:T(8,128)S(1)}, f32[128,256]{1,0:T(8,128)}, u32[]{:S(2)}) copy-start(f32[128,256]{1,0:T(8,128)} %param.11) | copy-start | bytes 393220
  103.9 654.2 %copy-start.7 = (f32[128]{0:T(128)S(1)}, f32[128]{0:T(128)}, u32[]{:S(2)}) copy-start(f32[128]{0:T(128)} %param.13) | copy-start | bytes 1540
  103.9 810.3 %all-reduce.3.cloned.1.call-start = ((), (), s32[]{:S(2)}) async-start(), calls=%async_computation.3 | async-start | bytes 4718592 | tf_op jit(solution)/shard_map/psum | solution.py:69
Sparse Core Ops, SparseCore 0:
  15.4 71.3 all-gather.3
  104.0 648.8 reduce-scatter.1
  759.3 154.9 all-reduce.2
where the time goes:
time: 934 us; the launch traced here: 933 us
  waiting for transfers between devices  726 us (78%)
  blocking collectives  142 us (15%)
  matrix products  29.3 us (3%)
  between operations  15.7 us (2%)
  local copies, waits for them, and re-layouts  12.9 us (1%)
    reduce_scatter x1, waiting for transfers between devices, device_step(): lax.psum_scatter(item_part, 'dp', scatter_dimension=0, tiled=True)  641 us
    psum x1, waiting for transfers between devices, device_step(): lax.psum((jnp.sum(log_norm - pos_score),) + user_grads + item_grads, 'dp')  85.1 us
    psum x1, blocking collectives, device_step(): lax.psum((jnp.sum(log_norm - pos_score),) + user_grads + item_grads, 'dp')  69.7 us
    all_gather x1, blocking collectives, device_step(): logq_all = lax.all_gather(log_q, 'dp', axis=0, tiled=True)  38.8 us
    all_gather x1, blocking collectives, device_step(): id_all = lax.all_gather(item_id, 'dp', axis=0, tiled=True)  33.3 us
  transfers between devices with their start and end apart: 3, of which 2 were waited for; matrix products, arithmetic and copies ran while one was open for 1% of the time, Pallas kernels for 0%

commit v1 on v0

v1 whole, which is shorter than its diff:
```python
import functools

import jax
import jax.numpy as jnp
from jax import lax
from jax.experimental import pallas as pl
from jax.experimental.pallas import tpu as pltpu
from jax.sharding import PartitionSpec as P

MESH = pl.DeviceIdType.MESH
F32 = jnp.float32
BF16 = jnp.bfloat16
INV_TEMP = 1.0 / 0.05
NORM_EPS = 1e-6
ROWS = 128
EMB = 128
WIDE = 384
IN_WIDTH = 256
NEG = -3.0e38
GRIDS = {128: (4, 4, 4, 2), 16: (2, 2, 2, 2)}
AZ, AY, AX, AK = range(4)
C00 = (((0,), (0,)), ((), ()))
C11 = (((1,), (1,)), ((), ()))
C10 = (((1,), (0,)), ((), ()))
N_REMOTE = 176


def mm(a, b, dims=C10):
    return lax.dot_general(a, b, dims, preferred_element_type=F32)


def scratch_table(nz, ny, nx, nk):
    n_plane, n_small = nz * ny, nk * nx
    n_tile = n_plane // 2
    n_query = n_small * ROWS
    n_wide = n_plane * ROWS
    longest = max(n_wide, n_query)
    turns = ((nx, ny, nz), (ny, nz, nx), (nz, nx, ny))

    def vm(dtype, *shape):
        return pltpu.VMEM(shape, dtype)

    def two(dtype, *shape):
        return [vm(dtype, *shape) for _ in range(2)]

    def six(shape_of):
        return [[vm(F32, *shape_of(*turn), WIDE) for turn in turns] for _ in range(2)]

    return dict(
        xf=two(F32, ROWS, IN_WIDTH),
        wf=[[vm(F32, IN_WIDTH, WIDE), vm(F32, WIDE, WIDE), vm(F32, WIDE, EMB)] for _ in range(2)],
        wh=[[vm(BF16, IN_WIDTH, WIDE), vm(BF16, WIDE, WIDE), vm(BF16, WIDE, EMB)] for _ in range(2)],
        xt=two(BF16, IN_WIDTH, ROWS),
        h1=two(BF16, ROWS, WIDE),
        h2=two(BF16, ROWS, WIDE),
        h1t=two(BF16, WIDE, ROWS),
        h2t=two(BF16, WIDE, ROWS),
        unit=two(F32, ROWS, EMB),
        inv=two(F32, ROWS, EMB),
        plane=two(BF16, nz, ny, ROWS, EMB),
        small=two(BF16, nk, nx, ROWS, EMB),
        parts=two(F32, n_small, ROWS, EMB),
        from_core=two(F32, nx, ROWS, EMB),
        core_sum=two(F32, nx, ROWS, EMB),
        from_x=two(F32, nx - 1, ROWS, EMB),
        dw=two(F32, nk, 3, ROWS, WIDE),
        from_pair=two(F32, 3, ROWS, WIDE),
        pair_sum=two(F32, 3, ROWS, WIDE),
        ra=six(lambda a, b, c: (a - 1, ROWS // a)),
        sa=six(lambda a, b, c: (ROWS // a,)),
        rb=six(lambda a, b, c: (b - 1, ROWS // a // b)),
        cx=six(lambda a, b, c: (c, ROWS // a // b)),
        res=vm(F32, nk, 2, 3, ROWS, WIDE),
        meta_plane=vm(F32, nz, ny, 8, ROWS),
        meta_small=vm(F32, nk, nx, 8, ROWS),
        lqc_plane=vm(F32, n_plane, ROWS, ROWS),
        idc_plane=vm(jnp.int32, n_plane, ROWS, ROWS),
        lqc_small=vm(F32, n_small, ROWS, ROWS),
        idc_small=vm(jnp.int32, n_small, ROWS, ROWS),
        idr_plane=vm(jnp.int32, 1, n_wide),
        idr_small=vm(jnp.int32, 1, n_query),
        probs=vm(F32, n_tile, 256, n_query),
        tile_max=vm(F32, n_tile, 1, n_query),
        tile_sum=vm(F32, n_tile, 1, n_query),
        factor=vm(F32, n_tile, 1, n_query),
        stats=vm(F32, nk, nx, 2 * n_small, ROWS),
        stat_all=vm(F32, 2 * n_small, ROWS),
        plane_t=vm(BF16, EMB, n_wide),
        grad_tile=vm(BF16, n_wide, 256),
        scores=vm(F32, n_small // 2, 256, n_wide),
        row_max=vm(F32, 1, longest),
        row_inv=vm(F32, 1, longest),
        ml=vm(F32, nz, ny, 8, ROWS),
        lx=vm(F32, nk, nx, 8, ROWS),
        own_diag=vm(BF16, ROWS, ROWS),
        pos=vm(F32, 1, ROWS),
        send_sem=pltpu.SemaphoreType.DMA((N_REMOTE,)),
        recv_sem=pltpu.SemaphoreType.DMA((N_REMOTE,)),
        load_sem=pltpu.SemaphoreType.DMA((8,)),
    )


class Space:
    def __init__(self, entries):
        self.__dict__.update(entries)


def step_kernel(grid, tree, *refs):
    nz, ny, nx, nk = grid
    n_plane, n_small = nz * ny, nk * nx
    n_tile = n_plane // 2
    n_chunk = n_small // 2
    n_query = n_small * ROWS
    n_wide = n_plane * ROWS
    batch = float(nz * ny * nx * nk * ROWS)
    x_in, lq_in, id_in = refs[0:2], refs[2], refs[3]
    w_in = (refs[4:7], refs[7:10])
    out_ref, loss_ref = refs[10:12]
    s = Space(jax.tree.unflatten(tree, refs[12:]))

    me = lax.axis_index('dp')
    size = grid
    stride = (ny * nx * nk, nx * nk, nk, 1)
    co = tuple(lax.rem(me // stride[ax], size[ax]) for ax in range(4))
    z, y, x, k = co

    def wrap(ax, r):
        return lax.rem(co[ax] + r, size[ax])

    def at_peer(ax, r):
        return me + (wrap(ax, r) - co[ax]) * stride[ax]

    def order(n):
        return sorted(range(1, n), key=lambda r: min(r, n - r))

    used = [0]
    started = []

    class Exchange:
        def __init__(self, peers):
            self.peers = peers
            self.base = used[0]
            used[0] += len(peers)
            self.copies = []

        def send(self, src, dst):
            for i, (r, dest, dev) in enumerate(self.peers):
                copy = pltpu.make_async_remote_copy(
                    src_ref=src(r, dest), dst_ref=dst(r, dest),
                    send_sem=s.send_sem.at[self.base + i], recv_sem=s.recv_sem.at[self.base + i],
                    device_id=(dev,), device_id_type=MESH)
                copy.start()
                self.copies.append(copy)
                started.append(copy)
            return self

        def recv(self):
            for copy in self.copies:
                copy.wait_recv()

    def along(ax):
        return Exchange([(r, wrap(ax, r), at_peer(ax, r)) for r in order(size[ax])])

    def share(ax, ref):
        return along(ax).send(lambda r, d: ref, lambda r, d: ref)

    def small_group():
        peers = []
        for rk in range(nk):
            for rx in [0] + order(nx):
                if rk or rx:
                    dev = me + (wrap(AK, rk) - k) + (wrap(AX, rx) - x) * nk
                    peers.append((len(peers), None, dev))
        return Exchange(peers)

    loads = []

    def load(src, dst):
        copy = pltpu.make_async_copy(src, dst, s.load_sem.at[len(loads)])
        copy.start()
        loads.append(copy)
        return copy

    load_x, load_w = {}, {}
    for t in (1, 0):
        load_x[t] = load(x_in[t], s.xf[t])
        load_w[t] = [load(w_in[t][i], s.wf[t][i]) for i in range(3)]

    barrier = pltpu.get_barrier_semaphore()
    greet = [at_peer(ax, r) for ax in (AZ, AY, AX, AK) for r in range(1, size[ax])]
    greet += [me + (wrap(AK, rk) - k) + (wrap(AX, rx) - x) * nk for rk in range(1, nk) for rx in range(1, nx)]
    for dev in greet:
        pl.semaphore_signal(barrier, inc=1, device_id=(dev,), device_id_type=MESH)

    ids = id_in[...]
    zero_row = jnp.zeros((1, ROWS), F32)
    meta = jnp.concatenate([lq_in[...], lax.shift_right_logical(ids, 16).astype(F32),
                            lax.bitwise_and(ids, 65535).astype(F32)] + [zero_row] * 5, axis=0)
    s.meta_plane[z, y] = meta
    s.meta_small[k, x] = meta

    def forward(t):
        load_x[t].wait()
        xb = s.xf[t][...].astype(BF16)
        for i in range(3):
            load_w[t][i].wait()
            s.wh[t][i][...] = s.wf[t][i][...].astype(BF16)
        act = jnp.maximum(mm(xb, s.wh[t][0][...]), 0.0).astype(BF16)
        s.h1[t][...] = act
        act = jnp.maximum(mm(act, s.wh[t][1][...]), 0.0).astype(BF16)
        s.h2[t][...] = act
        raw = mm(act, s.wh[t][2][...])
        inv = lax.rsqrt(jnp.sum(raw * raw, axis=1, keepdims=True) + NORM_EPS)
        unit = raw * inv
        s.unit[t][...] = unit
        s.inv[t][...] = jnp.broadcast_to(inv, (ROWS, EMB))
        half = unit.astype(BF16)
        s.plane[t][z, y] = half
        s.small[t][k, x] = half

    half_rows = ROWS // 2
    top, low = pl.ds(0, half_rows), pl.ds(half_rows, half_rows)

    def plane_first(t):
        ref = s.plane[t]
        return share(AY, ref.at[z, y, top]), share(AZ, ref.at[z, y, low])

    def plane_second(t, first):
        ref = s.plane[t]
        first[0].recv()
        a = share(AZ, ref.at[z, :, top])
        first[1].recv()
        b = share(AY, ref.at[:, y, low])
        return a, b

    forward(1)
    pl.semaphore_wait(barrier, len(greet))
    v_first = plane_first(1)
    v_small = share(AX, s.small[1].at[k, x])
    meta_y = share(AY, s.meta_plane.at[z, y])
    meta_x = share(AX, s.meta_small.at[k, x])
    forward(0)
    u_small = share(AX, s.small[0].at[k, x])
    v_second = plane_second(1, v_first)
    u_first = plane_first(0)
    meta_y.recv()
    meta_z = share(AZ, s.meta_plane.at[z])
    meta_x.recv()
    meta_k = share(AK, s.meta_small.at[k])
    u_small.recv()
    u_small_k = share(AK, s.small[0].at[k])
    v_small.recv()
    v_small_k = share(AK, s.small[1].at[k])
    u_second = plane_second(0, u_first)

    def columns(ref, lq_out, id_out, id_row, count):
        flat = ref[...].reshape(count * 8, ROWS)
        if count * 8 < ROWS:
            flat = jnp.concatenate([flat, jnp.zeros((ROWS - count * 8, ROWS), F32)], axis=0)
        turned = flat.T
        for i in range(count):
            lq_out[i] = jnp.broadcast_to(turned[:, 8 * i:8 * i + 1], (ROWS, ROWS))
            hi = turned[:, 8 * i + 1:8 * i + 2].astype(jnp.int32)
            lo = turned[:, 8 * i + 2:8 * i + 3].astype(jnp.int32)
            id_out[i] = jnp.broadcast_to(hi * 65536 + lo, (ROWS, ROWS))
            row_hi = flat[8 * i + 1:8 * i + 2].astype(jnp.int32)
            row_lo = flat[8 * i + 2:8 * i + 3].astype(jnp.int32)
            id_row[:, i * ROWS:(i + 1) * ROWS] = row_hi * 65536 + row_lo

    meta_k.recv()
    columns(s.meta_small, s.lqc_small, s.idc_small, s.idr_small, n_small)
    meta_z.recv()
    columns(s.meta_plane, s.lqc_plane, s.idc_plane, s.idr_plane, n_plane)

    def transposed(value):
        return value.astype(F32).T.astype(BF16)

    for t in (0, 1):
        s.xt[t][...] = s.xf[t][...].T.astype(BF16)
        s.h1t[t][...] = transposed(s.h1[t][...])
        s.h2t[t][...] = transposed(s.h2[t][...])

    v_own = s.small[1][k, x]
    u_own = s.small[0][k, x]
    eye = (lax.broadcasted_iota(jnp.int32, (ROWS, ROWS), 0) == lax.broadcasted_iota(jnp.int32, (ROWS, ROWS), 1))
    own_scores = mm(v_own, u_own, C11) * INV_TEMP - s.lqc_small[k * nx + x]
    s.pos[...] = jnp.sum(jnp.where(eye, own_scores, 0.0), axis=0, keepdims=True)

    u_small_k.recv()
    for part in v_second:
        part.recv()

    per_z = ny // 2

    def twice(value):
        return jnp.concatenate([value, value], axis=1)

    def score_tile(tile, carry):
        items = s.plane[1][tile // per_z, pl.ds(lax.rem(tile, per_z) * 2, 2)].reshape(256, EMB)
        lq_wide = twice(s.lqc_plane[pl.ds(tile * 2, 2)].reshape(256, ROWS))
        id_wide = twice(s.idc_plane[pl.ds(tile * 2, 2)].reshape(256, ROWS))
        for n in range(n_chunk):
            lanes = slice(n * 256, (n + 1) * 256)
            queries = s.small[0][2 * n // nx, pl.ds(2 * n % nx, 2)].reshape(256, EMB)
            score = mm(items, queries, C11) * INV_TEMP - lq_wide
            score = jnp.where(id_wide == s.idr_small[:, lanes], -jnp.inf, score)
            peak = jnp.maximum(jnp.max(score, axis=0, keepdims=True), NEG)
            prob = jnp.exp(score - peak)
            s.probs[tile, :, lanes] = prob
            s.tile_max[tile, :, lanes] = peak
            s.tile_sum[tile, :, lanes] = jnp.sum(prob, axis=0, keepdims=True)
        return carry

    lax.fori_loop(0, n_tile, score_tile, 0)

    tile_max = s.tile_max[...]
    part_max = jnp.max(tile_max, axis=0)
    part_sum = jnp.sum(s.tile_sum[...] * jnp.exp(tile_max - part_max[None]), axis=0)
    for i in range(n_small):
        s.stats[k, x, i:i + 1] = part_max[:, i * ROWS:(i + 1) * ROWS]
        s.stats[k, x, n_small + i:n_small + i + 1] = part_sum[:, i * ROWS:(i + 1) * ROWS]
    own_block = k * nx + x
    pos = s.pos[...]
    old_max = s.stats[k, x, pl.ds(own_block, 1)]
    new_max = jnp.maximum(old_max, pos)
    s.stats[k, x, pl.ds(own_block, 1)] = new_max
    s.stats[k, x, pl.ds(n_small + own_block, 1)] = (
        s.stats[k, x, pl.ds(n_small + own_block, 1)] * jnp.exp(old_max - new_max) + jnp.exp(pos - new_max))
    stats_ref = s.stats.at[k, x]
    stats = small_group().send(lambda r, d: stats_ref, lambda r, d: stats_ref)

    for iz in range(nz):
        for iy in range(ny):
            i = iz * ny + iy
            s.plane_t[:, i * ROWS:(i + 1) * ROWS] = transposed(s.plane[1][iz, iy])

    v_small_k.recv()
    for part in u_second:
        part.recv()

    def wide_tile(chunk, carry):
        first = 2 * chunk
        items = s.small[1][first // nx, pl.ds(lax.rem(first, nx), 2)].reshape(256, EMB)
        lq_wide = twice(s.lqc_small[pl.ds(first, 2)].reshape(256, ROWS))
        id_wide = twice(s.idc_small[pl.ds(first, 2)].reshape(256, ROWS))
        for n in range(n_tile):
            lanes = slice(n * 256, (n + 1) * 256)
            queries = s.plane[0][2 * n // ny, pl.ds(2 * n % ny, 2)].reshape(256, EMB)
            score = mm(items, queries, C11) * INV_TEMP - lq_wide
            s.scores[chunk, :, lanes] = jnp.where(id_wide == s.idr_plane[:, lanes], -jnp.inf, score)
        return carry

    lax.fori_loop(0, n_chunk, wide_tile, 0)

    stats.recv()
    every = s.stats[...].reshape(n_small, 2 * n_small, ROWS)
    all_max = jnp.max(every[:, :n_small], axis=0)
    all_sum = jnp.zeros_like(all_max)
    for i in range(n_small):
        all_sum = all_sum + every[i, n_small:] * jnp.exp(every[i, :n_small] - all_max)
    all_inv = 1.0 / (all_sum * batch)
    s.stat_all[:n_small] = all_max
    s.stat_all[n_small:] = all_sum
    for i in range(n_small):
        s.row_max[:, i * ROWS:(i + 1) * ROWS] = all_max[i:i + 1]
        s.row_inv[:, i * ROWS:(i + 1) * ROWS] = all_inv[i:i + 1]
    own_max = s.stat_all[pl.ds(own_block, 1)]
    own_sum = s.stat_all[pl.ds(n_small + own_block, 1)]
    s.ml[z, y] = jnp.concatenate([own_max, own_sum, pos] + [zero_row] * 5, axis=0)
    ml_y = share(AY, s.ml.at[z, y])
    own_grad = (jnp.exp(pos - own_max) / own_sum - 1.0) / batch
    s.own_diag[...] = jnp.where(eye, jnp.broadcast_to(own_grad, (ROWS, ROWS)), 0.0).astype(BF16)

    s.factor[...] = (jnp.exp(tile_max - s.row_max[:, :n_query][None]) * s.row_inv[:, :n_query][None])

    def user_chunk(index, carry):
        chunk = lax.rem((1 - k) * (n_chunk // 2) + index, n_chunk)
        lanes = pl.ds(pl.multiple_of(chunk * 256, 256), 256)
        for tile in range(n_tile):
            s.grad_tile[tile * 256:(tile + 1) * 256] = (
                s.probs[tile, :, lanes] * s.factor[tile, :, lanes]).astype(BF16)
        turned = mm(s.plane_t[...], s.grad_tile[...])
        s.parts[0][2 * chunk] = turned[:, :ROWS]
        s.parts[0][2 * chunk + 1] = turned[:, ROWS:]
        return carry

    def to_partner(t):
        ref = s.parts[t]
        into = s.from_core[t]
        return along(AK).send(lambda r, d: ref.at[pl.ds((1 - k) * nx, nx)], lambda r, d: into)

    def to_x(t, exchange):
        exchange.recv()
        for i in range(nx):
            s.core_sum[t][i] = s.parts[t][k * nx + i] + s.from_core[t][i]
        return along(AX).send(lambda r, d: s.core_sum[t].at[d], lambda r, d: s.from_x[t].at[r - 1])

    def summed(t, exchange):
        exchange.recv()
        total = s.core_sum[t][x]
        for r in range(1, nx):
            total = total + s.from_x[t][r - 1]
        return total * INV_TEMP

    lax.fori_loop(0, n_chunk // 2, user_chunk, 0)
    du_core = to_partner(0)
    lax.fori_loop(n_chunk // 2, n_chunk, user_chunk, 0)
    ml_y.recv()
    ml_z = share(AZ, s.ml.at[z])
    s.parts[0][own_block] = s.parts[0][own_block] + mm(v_own, s.own_diag[...], C00)
    du_x = to_x(0, du_core)

    ml_z.recv()
    loss_row = jnp.zeros((1, ROWS), F32)
    for iz in range(nz):
        for iy in range(ny):
            i = iz * ny + iy
            row = s.ml[iz, iy]
            s.row_max[:, i * ROWS:(i + 1) * ROWS] = row[0:1]
            s.row_inv[:, i * ROWS:(i + 1) * ROWS] = 1.0 / (row[1:2] * batch)
            loss_row = loss_row + ((row[0:1] - row[2:3]) + jnp.log(row[1:2]))
    s.lx[k, x] = jnp.broadcast_to(loss_row, (8, ROWS))
    lx_ref = s.lx.at[k, x]
    loss_x = small_group().send(lambda r, d: lx_ref, lambda r, d: lx_ref)

    def item_chunk(index, carry):
        chunk = lax.rem((1 - k) * (n_chunk // 2) + index, n_chunk)
        total = jnp.zeros((256, EMB), F32)
        grads = []
        for n in range(n_tile):
            lanes = slice(n * 256, (n + 1) * 256)
            grads.append((jnp.exp(s.scores[chunk, :, lanes] - s.row_max[:, lanes])
                          * s.row_inv[:, lanes]).astype(BF16))
        total = mm(jnp.concatenate(grads, axis=1), s.plane[0][...].reshape(n_wide, EMB))
        s.parts[1][2 * chunk] = total[:ROWS]
        s.parts[1][2 * chunk + 1] = total[ROWS:]
        return carry

    lax.fori_loop(0, n_chunk // 2, item_chunk, 0)
    dv_core = to_partner(1)
    lax.fori_loop(n_chunk // 2, n_chunk, item_chunk, 0)
    s.parts[1][own_block] = s.parts[1][own_block] + mm(s.own_diag[...], u_own)
    dv_x = to_x(1, dv_core)

    def backward(t, grad_unit):
        unit = s.unit[t][...]
        grad_raw = s.inv[t][...] * (grad_unit - unit * jnp.sum(unit * grad_unit, axis=1, keepdims=True))
        grad_half = grad_raw.astype(BF16)
        dw = s.dw[t]
        back = mm(grad_half, s.wh[t][2][...], C11)
        grad_two = jnp.where(s.h2[t][...] > 0, back, 0.0).astype(BF16)
        back = mm(grad_two, s.wh[t][1][...], C11)
        grad_one = jnp.where(s.h1[t][...] > 0, back, 0.0).astype(BF16)
        third = mm(s.h2t[t][...], grad_half)
        for i in range(3):
            dw[0, 2, :, i * EMB:(i + 1) * EMB] = third[i * ROWS:(i + 1) * ROWS]
        second = mm(s.h1t[t][...], grad_two)
        for i in range(3):
            dw[1, i] = second[i * ROWS:(i + 1) * ROWS]
        first = mm(s.xt[t][...], grad_one)
        for i in range(2):
            dw[0, i] = first[i * ROWS:(i + 1) * ROWS]

    axes = ((AX, AY, AZ), (AY, AZ, AX), (AZ, AX, AY))

    class WeightSum:
        def __init__(self, t):
            self.t = t

        def rows(self, q, deep):
            a, b, _ = axes[q]
            high = ROWS // size[a]
            if not deep:
                return pl.ds(pl.multiple_of(co[a] * high, high), high)
            step = high // size[b]
            return pl.ds(pl.multiple_of(co[a] * high + co[b] * step, step), step)

        def pair(self):
            ref, into = s.dw[self.t], s.from_pair[self.t]
            self.open = [along(AK).send(lambda r, d: ref.at[1 - k], lambda r, d: into)]

        def close(self):
            for exchange in self.open:
                exchange.recv()

        def scatter_one(self):
            self.close()
            self.open = []
            for q in range(3):
                total = s.pair_sum[self.t]
                total[q] = s.dw[self.t][k, q] + s.from_pair[self.t][q]
                high = ROWS // size[axes[q][0]]
                self.open.append(along(axes[q][0]).send(
                    lambda r, d, q=q, high=high: total.at[q, pl.ds(pl.multiple_of(d * high, high), high)],
                    lambda r, d, q=q: s.ra[self.t][q].at[r - 1]))

        def scatter_two(self):
            done, self.open = self.open, []
            for q in range(3):
                done[q].recv()
                value = s.pair_sum[self.t][q, self.rows(q, False)]
                for r in range(size[axes[q][0]] - 1):
                    value = value + s.ra[self.t][q][r]
                s.sa[self.t][q][...] = value
                step = ROWS // size[axes[q][0]] // size[axes[q][1]]
                self.open.append(along(axes[q][1]).send(
                    lambda r, d, q=q, step=step: s.sa[self.t][q].at[pl.ds(pl.multiple_of(d * step, step), step)],
                    lambda r, d, q=q: s.rb[self.t][q].at[r - 1]))

        def exchange_three(self):
            done, self.open = self.open, []
            for q in range(3):
                done[q].recv()
                a, b, c = axes[q]
                step = ROWS // size[a] // size[b]
                value = s.sa[self.t][q][pl.ds(pl.multiple_of(co[b] * step, step), step)]
                for r in range(size[b] - 1):
                    value = value + s.rb[self.t][q][r]
                s.cx[self.t][q][co[c]] = value
                self.open.append(share(c, s.cx[self.t][q].at[co[c]]))

        def gather_two(self):
            done, self.open = self.open, []
            for q in range(3):
                done[q].recv()
                value = s.cx[self.t][q][0]
                for r in range(1, size[axes[q][2]]):
                    value = value + s.cx[self.t][q][r]
                s.res[k, self.t, q, self.rows(q, True)] = value
                self.open.append(share(axes[q][1], s.res.at[k, self.t, q, self.rows(q, True)]))

        def gather_one(self):
            done, self.open = self.open, []
            for q in range(3):
                done[q].recv()
                self.open.append(share(axes[q][0], s.res.at[k, self.t, q, self.rows(q, False)]))

        def hand_over(self):
            done, self.open = self.open, []
            for q in range(3):
                done[q].recv()
                self.open.append(share(AK, s.res.at[k, self.t, q]))

    user, item = WeightSum(0), WeightSum(1)
    backward(0, summed(0, du_x).T)
    user.pair()
    user.scatter_one()
    backward(1, summed(1, dv_x))
    item.pair()
    user.scatter_two()
    item.scatter_one()
    user.exchange_three()
    item.scatter_two()
    user.gather_two()
    item.exchange_three()
    user.gather_one()
    item.gather_two()
    user.hand_over()
    item.gather_one()
    loss_x.recv()
    loss_total = jnp.zeros((8, ROWS), F32)
    for ik in range(nk):
        for ix in range(nx):
            loss_total = loss_total + s.lx[ik, ix]
    loss_ref[...] = loss_total
    user.close()
    out_ref[:, 0] = s.res[:, 0]
    item.hand_over()
    item.close()
    out_ref[:, 1] = s.res[:, 1]
    for copy in started:
        copy.wait_send()


def finish_kernel(batch, res_ref, loss_in, loss_ref, *outs):
    loss_ref[...] = jnp.sum(loss_in[0:1], axis=1, keepdims=True) / batch
    for t in range(2):
        one, two, three = outs[3 * t:3 * t + 3]
        for i in range(2):
            one[i * ROWS:(i + 1) * ROWS] = res_ref[0, t, i]
        for i in range(3):
            two[i * ROWS:(i + 1) * ROWS] = res_ref[1, t, i]
            three[i * ROWS:(i + 1) * ROWS] = res_ref[0, t, 2, :, i * EMB:(i + 1) * EMB]


def solution(mesh):
    devices = mesh.shape['dp']
    grid = GRIDS[devices]
    scratch, tree = jax.tree.flatten(scratch_table(*grid))
    vmem = pl.BlockSpec(memory_space=pltpu.VMEM)
    anywhere = pl.BlockSpec(memory_space=pl.ANY)

    def device_step(user_x, item_x, item_id, log_q, user_w1, user_w2, user_w3, item_w1, item_w2, item_w3):
        res, loss_rows = pl.pallas_call(
            functools.partial(step_kernel, grid, tree),
            out_shape=(jax.ShapeDtypeStruct((grid[3], 2, 3, ROWS, WIDE), F32), jax.ShapeDtypeStruct((8, ROWS), F32)),
            in_specs=[anywhere, anywhere, vmem, vmem] + [anywhere] * 6,
            out_specs=(vmem, vmem),
            scratch_shapes=scratch,
            compiler_params=pltpu.CompilerParams(collective_id=0, has_side_effects=True, vmem_limit_bytes=60 * 1024 * 1024),
            name='train_step',
        )(user_x, item_x, log_q.reshape(1, ROWS), item_id.reshape(1, ROWS), user_w1, user_w2, user_w3, item_w1, item_w2, item_w3)
        shapes = [(IN_WIDTH, WIDE), (WIDE, WIDE), (WIDE, EMB)] * 2
        outs = pl.pallas_call(
            functools.partial(finish_kernel, float(devices * ROWS)),
            out_shape=[jax.ShapeDtypeStruct((1, 1), F32)] + [jax.ShapeDtypeStruct(shape, F32) for shape in shapes],
            in_specs=[vmem, vmem],
            out_specs=[vmem] * 7,
            name='finish',
        )(res, loss_rows)
        return (outs[0].reshape(()),) + tuple(outs[1:])

    rows, vec, whole = P('dp', None), P('dp'), P()
    return jax.shard_map(device_step, mesh=mesh, in_specs=(rows, rows, vec, vec) + (whole,) * 6,
                         out_specs=(whole,) * 7, check_vma=False)
```

time: 934 us -> 77.5 us (0.08)
  waiting for transfers between devices: 726 us -> 0 us
  blocking collectives: 142 us -> 0 us
  Pallas kernels: 0 us -> 76.7 us
  matrix products: 29.3 us -> 0 us
  between operations: 15.7 us -> 0.64 us
  local copies, waits for them, and re-layouts: 12.9 us -> 0 us
    reduce_scatter x1 -> x0, waiting for transfers between devices: 641 us -> none  [device_step(): lax.psum_scatter(item_part, 'dp', scatter_dimension=0, tiled=True)]
    psum x1 -> x0, waiting for transfers between devices: 85.1 us -> none  [device_step(): lax.psum((jnp.sum(log_norm - pos_score),) + user_grads + item_grads, 'dp')]
    pallas_call x0 -> x2, Pallas kernels: none -> 76.7 us  [the longest x1 73.6 us: device_step(): pl.pallas_call(functools.partial(step_kernel, grid, tree), out_shape=(jax...]
    all_gather x2 -> x0, blocking collectives: 72.1 us -> none  [the longest x1 38.8 us: device_step(): logq_all = lax.all_gather(log_q, 'dp', axis=0, tiled=True)]
    psum x1 -> x0, blocking collectives: 69.7 us -> none  [device_step(): lax.psum((jnp.sum(log_norm - pos_score),) + user_grads + item_grads, 'dp')]
    dot_general x17 -> x0, matrix products: 29.3 us -> none  [the longest x1 5.8 us: device_step(): lax.dot_general(user_half, item_all, COL_DIMS, preferred_element_type=jnp...]
    unnamed x22 -> x0, local copies, waits for them, and re-layouts: 12.9 us -> none
  transfers between devices with their start and end apart: 3 -> 0, of which waited for: 2 -> 0; matrix products, arithmetic and copies ran while one was open for 1% -> 0% of each run, Pallas kernels for 0% -> 0%
where the time goes in v1:
time: 77.5 us; the launch traced here: 77.3 us
  Pallas kernels  76.7 us (99%)
    pallas_call x1, Pallas kernels, device_step(): pl.pallas_call(functools.partial(step_kernel, grid, tree), out_shape=(jax...  73.6 us
    pallas_call x1, Pallas kernels, device_step(): pl.pallas_call(functools.partial(finish_kernel, float(devices * ROWS)), o...  3.09 us

profile of v1, /device:TPU:1, one launch (start us, length us, event | category | flops | bytes accessed | tf_op | source)
XLA Modules:
  0.0 77.3 jit_solution(16092606064713815398)
XLA Ops:
  0.6 73.6 %train_step.1 = (f32[2,2,3,128,384]{4,3,2,1,0:T(8,128)}, f32[8,128]{1,0:T(8,128)}) custom-call(f32[128,256]{1,0:T(8,128)} %refs_0_.1, f32[128,256]{1,0:T(8,128)} %refs_1_.1, f32[1,128]{1,0:T(1,128)} %bitcast.3, s32[1,128]{1,0:T(1,128)} %bitcast.4, f32[256,384]{1,0:T(8,128)} %refs_4_.1, f32[384,384]{1,0:T(8,128)} %refs_5_.1, f32[384,128]{1,0:T(8,128)} %refs_6_.1, ...), custom_call_target="tpu_custom_call" | custom-call | tf_op jit(solution)/shard_map/train_step/pallas_call | solution.py:594
  74.2 3.1 %finish.1 = (f32[1,1]{1,0:T(1,128)}, f32[256,384]{1,0:T(8,128)}, f32[384,384]{1,0:T(8,128)}, f32[384,128]{1,0:T(8,128)}, f32[256,384]{1,0:T(8,128)}, /*index=5*/f32[384,384]{1,0:T(8,128)}, f32[384,128]{1,0:T(8,128)}) custom-call(f32[2,2,3,128,384]{4,3,2,1,0:T(8,128)} %get-tuple-element.16.res_ref, f32[8,128]{1,0:T(8,128)} %get-tuple-element.17.loss_in), custom_call_target="tpu_custom_call" | custom-call | tf_op jit(solution)/shard_map/finish/pallas_call | solution.py:604

commit v2 on v1

--- a/solution.py
+++ b/solution.py
@@ -22,7 +22,7 @@
 C00 = (((0,), (0,)), ((), ()))
 C11 = (((1,), (1,)), ((), ()))
 C10 = (((1,), (0,)), ((), ()))
-N_REMOTE = 176
+N_REMOTE = 192
 
 
 def mm(a, b, dims=C10):
@@ -31,7 +31,7 @@
 
 def scratch_table(nz, ny, nx, nk):
     n_plane, n_small = nz * ny, nk * nx
-    n_tile = n_plane // 2
+    n_tile, tile_rows = nz + ny, ny * ROWS // 2
     n_query = n_small * ROWS
     n_wide = n_plane * ROWS
     longest = max(n_wide, n_query)
@@ -70,16 +70,15 @@
         sa=six(lambda a, b, c: (ROWS // a,)),
         rb=six(lambda a, b, c: (b - 1, ROWS // a // b)),
         cx=six(lambda a, b, c: (c, ROWS // a // b)),
-        res=vm(F32, nk, 2, 3, ROWS, WIDE),
         meta_plane=vm(F32, nz, ny, 8, ROWS),
         meta_small=vm(F32, nk, nx, 8, ROWS),
-        lqc_plane=vm(F32, n_plane, ROWS, ROWS),
-        idc_plane=vm(jnp.int32, n_plane, ROWS, ROWS),
+        lqc_plane=vm(F32, nz, ny, ROWS, ROWS),
+        idc_plane=vm(jnp.int32, nz, ny, ROWS, ROWS),
         lqc_small=vm(F32, n_small, ROWS, ROWS),
         idc_small=vm(jnp.int32, n_small, ROWS, ROWS),
         idr_plane=vm(jnp.int32, 1, n_wide),
         idr_small=vm(jnp.int32, 1, n_query),
-        probs=vm(F32, n_tile, 256, n_query),
+        probs=vm(F32, n_tile, tile_rows, n_query),
         tile_max=vm(F32, n_tile, 1, n_query),
         tile_sum=vm(F32, n_tile, 1, n_query),
         factor=vm(F32, n_tile, 1, n_query),
@@ -108,7 +107,7 @@
 def step_kernel(grid, tree, *refs):
     nz, ny, nx, nk = grid
     n_plane, n_small = nz * ny, nk * nx
-    n_tile = n_plane // 2
+    n_tile, tile_rows = nz + ny, ny * ROWS // 2
     n_chunk = n_small // 2
     n_query = n_small * ROWS
     n_wide = n_plane * ROWS
@@ -135,28 +134,38 @@
 
     used = [0]
     started = []
+    drained = [0]
 
     class Exchange:
         def __init__(self, peers):
             self.peers = peers
             self.base = used[0]
             used[0] += len(peers)
-            self.copies = []
+            self.copies = {}
+
+        def post(self, index, src, dst):
+            copy = pltpu.make_async_remote_copy(
+                src_ref=src, dst_ref=dst,
+                send_sem=s.send_sem.at[self.base + index], recv_sem=s.recv_sem.at[self.base + index],
+                device_id=(self.peers[index][2],), device_id_type=MESH)
+            copy.start()
+            self.copies[index] = copy
+            started.append(copy)
 
         def send(self, src, dst):
             for i, (r, dest, dev) in enumerate(self.peers):
-                copy = pltpu.make_async_remote_copy(
-                    src_ref=src(r, dest), dst_ref=dst(r, dest),
-                    send_sem=s.send_sem.at[self.base + i], recv_sem=s.recv_sem.at[self.base + i],
-                    device_id=(dev,), device_id_type=MESH)
-                copy.start()
-                self.copies.append(copy)
-                started.append(copy)
+                self.post(i, src(r, dest), dst(r, dest))
             return self
 
         def recv(self):
-            for copy in self.copies:
+            for copy in self.copies.values():
                 copy.wait_recv()
+
+        def one(self, index, view):
+            return pltpu.make_async_remote_copy(
+                src_ref=view, dst_ref=view,
+                send_sem=s.send_sem.at[self.base + index], recv_sem=s.recv_sem.at[self.base + index],
+                device_id=(self.peers[0][2],), device_id_type=MESH)
 
     def along(ax):
         return Exchange([(r, wrap(ax, r), at_peer(ax, r)) for r in order(size[ax])])
@@ -173,6 +182,19 @@
                     peers.append((len(peers), None, dev))
         return Exchange(peers)
 
+    def plane_group():
+        peers = []
+        for rz in [0] + order(nz):
+            for ry in [0] + order(ny):
+                if rz or ry:
+                    peers.append((len(peers), None, me + (wrap(AZ, rz) - z) * stride[AZ] + (wrap(AY, ry) - y) * stride[AY]))
+        return Exchange(peers)
+
+    def drain(upto):
+        while drained[0] < upto:
+            started[drained[0]].wait_send()
+            drained[0] += 1
+
     loads = []
 
     def load(src, dst):
@@ -189,6 +211,7 @@
     barrier = pltpu.get_barrier_semaphore()
     greet = [at_peer(ax, r) for ax in (AZ, AY, AX, AK) for r in range(1, size[ax])]
     greet += [me + (wrap(AK, rk) - k) + (wrap(AX, rx) - x) * nk for rk in range(1, nk) for rx in range(1, nx)]
+    greet += [me + (wrap(AZ, rz) - z) * stride[AZ] + (wrap(AY, ry) - y) * stride[AY] for rz in range(1, nz) for ry in range(1, ny)]
     for dev in greet:
         pl.semaphore_signal(barrier, inc=1, device_id=(dev,), device_id_type=MESH)
 
@@ -241,36 +264,37 @@
     meta_x = share(AX, s.meta_small.at[k, x])
     forward(0)
     u_small = share(AX, s.small[0].at[k, x])
+    u_first = plane_first(0)
     v_second = plane_second(1, v_first)
-    u_first = plane_first(0)
     meta_y.recv()
     meta_z = share(AZ, s.meta_plane.at[z])
     meta_x.recv()
     meta_k = share(AK, s.meta_small.at[k])
     u_small.recv()
     u_small_k = share(AK, s.small[0].at[k])
+    u_second = plane_second(0, u_first)
     v_small.recv()
     v_small_k = share(AK, s.small[1].at[k])
-    u_second = plane_second(0, u_first)
-
-    def columns(ref, lq_out, id_out, id_row, count):
+    gathers = len(started)
+
+    def columns(ref, lq_out, id_out, id_row, count, nested):
         flat = ref[...].reshape(count * 8, ROWS)
         if count * 8 < ROWS:
             flat = jnp.concatenate([flat, jnp.zeros((ROWS - count * 8, ROWS), F32)], axis=0)
         turned = flat.T
         for i in range(count):
-            lq_out[i] = jnp.broadcast_to(turned[:, 8 * i:8 * i + 1], (ROWS, ROWS))
+            lq_out[divmod(i, nested) if nested else i] = jnp.broadcast_to(turned[:, 8 * i:8 * i + 1], (ROWS, ROWS))
             hi = turned[:, 8 * i + 1:8 * i + 2].astype(jnp.int32)
             lo = turned[:, 8 * i + 2:8 * i + 3].astype(jnp.int32)
-            id_out[i] = jnp.broadcast_to(hi * 65536 + lo, (ROWS, ROWS))
+            id_out[divmod(i, nested) if nested else i] = jnp.broadcast_to(hi * 65536 + lo, (ROWS, ROWS))
             row_hi = flat[8 * i + 1:8 * i + 2].astype(jnp.int32)
             row_lo = flat[8 * i + 2:8 * i + 3].astype(jnp.int32)
             id_row[:, i * ROWS:(i + 1) * ROWS] = row_hi * 65536 + row_lo
 
     meta_k.recv()
-    columns(s.meta_small, s.lqc_small, s.idc_small, s.idr_small, n_small)
+    columns(s.meta_small, s.lqc_small, s.idc_small, s.idr_small, n_small, 0)
     meta_z.recv()
-    columns(s.meta_plane, s.lqc_plane, s.idc_plane, s.idr_plane, n_plane)
+    columns(s.meta_plane, s.lqc_plane, s.idc_plane, s.idr_plane, n_plane, ny)
 
     def transposed(value):
         return value.astype(F32).T.astype(BF16)
@@ -287,18 +311,14 @@
     s.pos[...] = jnp.sum(jnp.where(eye, own_scores, 0.0), axis=0, keepdims=True)
 
     u_small_k.recv()
-    for part in v_second:
-        part.recv()
-
-    per_z = ny // 2
 
     def twice(value):
         return jnp.concatenate([value, value], axis=1)
 
-    def score_tile(tile, carry):
-        items = s.plane[1][tile // per_z, pl.ds(lax.rem(tile, per_z) * 2, 2)].reshape(256, EMB)
-        lq_wide = twice(s.lqc_plane[pl.ds(tile * 2, 2)].reshape(256, ROWS))
-        id_wide = twice(s.idc_plane[pl.ds(tile * 2, 2)].reshape(256, ROWS))
+    def score_tile(slot, items, lq_part, id_part):
+        s.plane_t[:, pl.ds(pl.multiple_of(slot * tile_rows, tile_rows), tile_rows)] = transposed(items)
+        lq_wide = twice(lq_part.reshape(tile_rows, ROWS))
+        id_wide = twice(id_part.reshape(tile_rows, ROWS))
         for n in range(n_chunk):
             lanes = slice(n * 256, (n + 1) * 256)
             queries = s.small[0][2 * n // nx, pl.ds(2 * n % nx, 2)].reshape(256, EMB)
@@ -306,12 +326,26 @@
             score = jnp.where(id_wide == s.idr_small[:, lanes], -jnp.inf, score)
             peak = jnp.maximum(jnp.max(score, axis=0, keepdims=True), NEG)
             prob = jnp.exp(score - peak)
-            s.probs[tile, :, lanes] = prob
-            s.tile_max[tile, :, lanes] = peak
-            s.tile_sum[tile, :, lanes] = jnp.sum(prob, axis=0, keepdims=True)
+            s.probs[slot, :, lanes] = prob
+            s.tile_max[slot, :, lanes] = peak
+            s.tile_sum[slot, :, lanes] = jnp.sum(prob, axis=0, keepdims=True)
+
+    def score_step(index, carry):
+        turn = jnp.where(index == 2, 3, jnp.where(index == 3, 2, index))
+        ref = s.plane[1]
+
+        @pl.when(index > 0)
+        def _():
+            for part, view in zip(v_second, (ref.at[z, :, top], ref.at[:, y, low])):
+                part.one(index - 1, view).wait_recv()
+
+        iz = lax.rem(z - turn + nz, nz)
+        iy = lax.rem(y - turn + ny, ny)
+        score_tile(2 * index, ref[iz, :, top].reshape(tile_rows, EMB), s.lqc_plane[iz, :, top], s.idc_plane[iz, :, top])
+        score_tile(2 * index + 1, ref[:, iy, low].reshape(tile_rows, EMB), s.lqc_plane[:, iy, low], s.idc_plane[:, iy, low])
         return carry
 
-    lax.fori_loop(0, n_tile, score_tile, 0)
+    lax.fori_loop(0, nz, score_step, 0)
 
     tile_max = s.tile_max[...]
     part_max = jnp.max(tile_max, axis=0)
@@ -329,21 +363,23 @@
     stats_ref = s.stats.at[k, x]
     stats = small_group().send(lambda r, d: stats_ref, lambda r, d: stats_ref)
 
-    for iz in range(nz):
-        for iy in range(ny):
-            i = iz * ny + iy
-            s.plane_t[:, i * ROWS:(i + 1) * ROWS] = transposed(s.plane[1][iz, iy])
-
     v_small_k.recv()
     for part in u_second:
         part.recv()
 
+    stages = ((2, 1), (3, 0)) if nx == 4 else ((1, 0),)
+
+    n_wide_tile = n_wide // 256
+
     def wide_tile(chunk, carry):
-        first = 2 * chunk
-        items = s.small[1][first // nx, pl.ds(lax.rem(first, nx), 2)].reshape(256, EMB)
-        lq_wide = twice(s.lqc_small[pl.ds(first, 2)].reshape(256, ROWS))
-        id_wide = twice(s.idc_small[pl.ds(first, 2)].reshape(256, ROWS))
-        for n in range(n_tile):
+        side = jnp.where(lax.rem(chunk, 2) == 0, 1 - k, k)
+        spots = []
+        for turns in zip(*stages):
+            spots.append(lax.rem(x + jnp.where(chunk // 2 == 0, turns[0], turns[-1]), nx))
+        items = jnp.concatenate([s.small[1][side, spot] for spot in spots], axis=0)
+        lq_wide = twice(jnp.concatenate([s.lqc_small[side * nx + spot] for spot in spots], axis=0))
+        id_wide = twice(jnp.concatenate([s.idc_small[side * nx + spot] for spot in spots], axis=0))
+        for n in range(n_wide_tile):
             lanes = slice(n * 256, (n + 1) * 256)
             queries = s.plane[0][2 * n // ny, pl.ds(2 * n % ny, 2)].reshape(256, EMB)
             score = mm(items, queries, C11) * INV_TEMP - lq_wide
@@ -367,7 +403,8 @@
     own_max = s.stat_all[pl.ds(own_block, 1)]
     own_sum = s.stat_all[pl.ds(n_small + own_block, 1)]
     s.ml[z, y] = jnp.concatenate([own_max, own_sum, pos] + [zero_row] * 5, axis=0)
-    ml_y = share(AY, s.ml.at[z, y])
+    ml_ref = s.ml.at[z, y]
+    ml_plane = plane_group().send(lambda r, d: ml_ref, lambda r, d: ml_ref)
     own_grad = (jnp.exp(pos - own_max) / own_sum - 1.0) / batch
     s.own_diag[...] = jnp.where(eye, jnp.broadcast_to(own_grad, (ROWS, ROWS)), 0.0).astype(BF16)
 
@@ -377,7 +414,7 @@
         chunk = lax.rem((1 - k) * (n_chunk // 2) + index, n_chunk)
         lanes = pl.ds(pl.multiple_of(chunk * 256, 256), 256)
         for tile in range(n_tile):
-            s.grad_tile[tile * 256:(tile + 1) * 256] = (
+            s.grad_tile[tile * tile_rows:(tile + 1) * tile_rows] = (
                 s.probs[tile, :, lanes] * s.factor[tile, :, lanes]).astype(BF16)
         turned = mm(s.plane_t[...], s.grad_tile[...])
         s.parts[0][2 * chunk] = turned[:, :ROWS]
@@ -405,12 +442,10 @@
     lax.fori_loop(0, n_chunk // 2, user_chunk, 0)
     du_core = to_partner(0)
     lax.fori_loop(n_chunk // 2, n_chunk, user_chunk, 0)
-    ml_y.recv()
-    ml_z = share(AZ, s.ml.at[z])
     s.parts[0][own_block] = s.parts[0][own_block] + mm(v_own, s.own_diag[...], C00)
     du_x = to_x(0, du_core)
-
-    ml_z.recv()
+    drain(gathers)
+    ml_plane.recv()
     loss_row = jnp.zeros((1, ROWS), F32)
     for iz in range(nz):
         for iy in range(ny):
@@ -423,24 +458,34 @@
     lx_ref = s.lx.at[k, x]
     loss_x = small_group().send(lambda r, d: lx_ref, lambda r, d: lx_ref)
 
-    def item_chunk(index, carry):
-        chunk = lax.rem((1 - k) * (n_chunk // 2) + index, n_chunk)
-        total = jnp.zeros((256, EMB), F32)
+    def item_chunk(stage, side, own):
+        chunk = 2 * stage + own
         grads = []
-        for n in range(n_tile):
+        for n in range(n_wide_tile):
             lanes = slice(n * 256, (n + 1) * 256)
             grads.append((jnp.exp(s.scores[chunk, :, lanes] - s.row_max[:, lanes])
                           * s.row_inv[:, lanes]).astype(BF16))
         total = mm(jnp.concatenate(grads, axis=1), s.plane[0][...].reshape(n_wide, EMB))
-        s.parts[1][2 * chunk] = total[:ROWS]
-        s.parts[1][2 * chunk + 1] = total[ROWS:]
-        return carry
-
-    lax.fori_loop(0, n_chunk // 2, item_chunk, 0)
-    dv_core = to_partner(1)
-    lax.fori_loop(n_chunk // 2, n_chunk, item_chunk, 0)
-    s.parts[1][own_block] = s.parts[1][own_block] + mm(s.own_diag[...], u_own)
-    dv_x = to_x(1, dv_core)
+        for i, r in enumerate(stages[stage]):
+            s.parts[1][side * nx + wrap(AX, r)] = total[i * ROWS:(i + 1) * ROWS]
+
+    dv_core = Exchange([(i, None, at_peer(AK, 1)) for i in range(nx)])
+    dv_x = along(AX)
+    for stage, turns in enumerate(stages):
+        item_chunk(stage, 1 - k, 0)
+        for i, r in enumerate(turns):
+            spot = wrap(AX, r)
+            dv_core.post(2 * stage + i, s.parts[1].at[(1 - k) * nx + spot], s.from_core[1].at[spot])
+        item_chunk(stage, k, 1)
+        if 0 in turns:
+            s.parts[1][own_block] = s.parts[1][own_block] + mm(s.own_diag[...], u_own)
+        for i, r in enumerate(turns):
+            spot = wrap(AX, r)
+            dv_core.copies[2 * stage + i].wait_recv()
+            s.core_sum[1][spot] = s.parts[1][k * nx + spot] + s.from_core[1][spot]
+            if r:
+                dv_x.post(order(nx).index(r), s.core_sum[1].at[spot], s.from_x[1].at[r - 1])
+    middle = len(started)
 
     def backward(t, grad_unit):
         unit = s.unit[t][...]
@@ -526,20 +571,20 @@
                 value = s.cx[self.t][q][0]
                 for r in range(1, size[axes[q][2]]):
                     value = value + s.cx[self.t][q][r]
-                s.res[k, self.t, q, self.rows(q, True)] = value
-                self.open.append(share(axes[q][1], s.res.at[k, self.t, q, self.rows(q, True)]))
+                out_ref[k, self.t, q, self.rows(q, True)] = value
+                self.open.append(share(axes[q][1], out_ref.at[k, self.t, q, self.rows(q, True)]))
 
         def gather_one(self):
             done, self.open = self.open, []
             for q in range(3):
                 done[q].recv()
-                self.open.append(share(axes[q][0], s.res.at[k, self.t, q, self.rows(q, False)]))
+                self.open.append(share(axes[q][0], out_ref.at[k, self.t, q, self.rows(q, False)]))
 
         def hand_over(self):
             done, self.open = self.open, []
             for q in range(3):
                 done[q].recv()
-                self.open.append(share(AK, s.res.at[k, self.t, q]))
+                self.open.append(share(AK, out_ref.at[k, self.t, q]))
 
     user, item = WeightSum(0), WeightSum(1)
     backward(0, summed(0, du_x).T)
@@ -547,16 +592,25 @@
     user.scatter_one()
     backward(1, summed(1, dv_x))
     item.pair()
+    drain(middle)
     user.scatter_two()
     item.scatter_one()
+    early = len(started)
     user.exchange_three()
     item.scatter_two()
+    drain(early)
+    early = len(started)
     user.gather_two()
     item.exchange_three()
+    drain(early)
+    early = len(started)
     user.gather_one()
     item.gather_two()
+    drain(early)
+    early = len(started)
     user.hand_over()
     item.gather_one()
+    drain(early)
     loss_x.recv()
     loss_total = jnp.zeros((8, ROWS), F32)
     for ik in range(nk):
@@ -564,12 +618,9 @@
             loss_total = loss_total + s.lx[ik, ix]
     loss_ref[...] = loss_total
     user.close()
-    out_ref[:, 0] = s.res[:, 0]
     item.hand_over()
     item.close()
-    out_ref[:, 1] = s.res[:, 1]
-    for copy in started:
-        copy.wait_send()
+    drain(len(started))
 
 
 def finish_kernel(batch, res_ref, loss_in, loss_ref, *outs):
@@ -588,13 +639,13 @@
     grid = GRIDS[devices]
     scratch, tree = jax.tree.flatten(scratch_table(*grid))
     vmem = pl.BlockSpec(memory_space=pltpu.VMEM)
-    anywhere = pl.BlockSpec(memory_space=pl.ANY)
+    hbm = pl.BlockSpec(memory_space=pltpu.HBM)
 
     def device_step(user_x, item_x, item_id, log_q, user_w1, user_w2, user_w3, item_w1, item_w2, item_w3):
         res, loss_rows = pl.pallas_call(
             functools.partial(step_kernel, grid, tree),
             out_shape=(jax.ShapeDtypeStruct((grid[3], 2, 3, ROWS, WIDE), F32), jax.ShapeDtypeStruct((8, ROWS), F32)),
-            in_specs=[anywhere, anywhere, vmem, vmem] + [anywhere] * 6,
+            in_specs=[hbm, hbm, vmem, vmem] + [hbm] * 6,
             out_specs=(vmem, vmem),
             scratch_shapes=scratch,
             compiler_params=pltpu.CompilerParams(collective_id=0, has_side_effects=True, vmem_limit_bytes=60 * 1024 * 1024),

time: 77.5 us -> 75.5 us (0.974)
  Pallas kernels: 76.7 us -> 74.7 us
    pallas_call x1, Pallas kernels: 73.6 us -> 71.6 us  [device_step(): pl.pallas_call(functools.partial(step_kernel, grid, tree), out_shape=(jax...]
where the time goes in v2:
time: 75.5 us; the launch traced here: 75.3 us
  Pallas kernels  74.7 us (99%)
    pallas_call x1, Pallas kernels, device_step(): pl.pallas_call(functools.partial(step_kernel, grid, tree), out_shape=(jax...  71.6 us
    pallas_call x1, Pallas kernels, device_step(): pl.pallas_call(functools.partial(finish_kernel, float(devices * ROWS)), o...  3.09 us

profile of v2, /device:TPU:1, one launch (start us, length us, event | category | flops | bytes accessed | tf_op | source)
XLA Modules:
  0.0 75.3 jit_solution(2582278098827193277)
XLA Ops:
  0.6 71.6 %train_step.1 = (f32[2,2,3,128,384]{4,3,2,1,0:T(8,128)}, f32[8,128]{1,0:T(8,128)}) custom-call(f32[128,256]{1,0:T(8,128)} %refs_0_.1, f32[128,256]{1,0:T(8,128)} %refs_1_.1, f32[1,128]{1,0:T(1,128)} %bitcast.3, s32[1,128]{1,0:T(1,128)} %bitcast.4, f32[256,384]{1,0:T(8,128)} %refs_4_.1, f32[384,384]{1,0:T(8,128)} %refs_5_.1, f32[384,128]{1,0:T(8,128)} %refs_6_.1, ...), custom_call_target="tpu_custom_call" | custom-call | tf_op jit(solution)/shard_map/train_step/pallas_call | solution.py:645
  72.2 3.1 %finish.1 = (f32[1,1]{1,0:T(1,128)}, f32[256,384]{1,0:T(8,128)}, f32[384,384]{1,0:T(8,128)}, f32[384,128]{1,0:T(8,128)}, f32[256,384]{1,0:T(8,128)}, /*index=5*/f32[384,384]{1,0:T(8,128)}, f32[384,128]{1,0:T(8,128)}) custom-call(f32[2,2,3,128,384]{4,3,2,1,0:T(8,128)} %get-tuple-element.16.res_ref, f32[8,128]{1,0:T(8,128)} %get-tuple-element.17.loss_in), custom_call_target="tpu_custom_call" | custom-call | tf_op jit(solution)/shard_map/finish/pallas_call | solution.py:655

commit v3 on v2

--- a/solution.py
+++ b/solution.py
@@ -43,18 +43,19 @@
     def two(dtype, *shape):
         return [vm(dtype, *shape) for _ in range(2)]
 
-    def six(shape_of):
-        return [[vm(F32, *shape_of(*turn), WIDE) for turn in turns] for _ in range(2)]
+    def each(shape_of):
+        return [vm(F32, *shape_of(*turn), WIDE) for turn in turns]
 
     return dict(
-        xf=two(F32, ROWS, IN_WIDTH),
-        wf=[[vm(F32, IN_WIDTH, WIDE), vm(F32, WIDE, WIDE), vm(F32, WIDE, EMB)] for _ in range(2)],
         wh=[[vm(BF16, IN_WIDTH, WIDE), vm(BF16, WIDE, WIDE), vm(BF16, WIDE, EMB)] for _ in range(2)],
-        xt=two(BF16, IN_WIDTH, ROWS),
         h1=two(BF16, ROWS, WIDE),
         h2=two(BF16, ROWS, WIDE),
-        h1t=two(BF16, WIDE, ROWS),
-        h2t=two(BF16, WIDE, ROWS),
+        xt=vm(BF16, 2, nk, IN_WIDTH, ROWS),
+        h1t=vm(BF16, 2, nk, WIDE, ROWS),
+        h2t=vm(BF16, 2, nk, WIDE, ROWS),
+        g1=vm(BF16, 2, nk, ROWS, WIDE),
+        g2=vm(BF16, 2, nk, ROWS, WIDE),
+        g3=vm(BF16, 2, nk, ROWS, EMB),
         unit=two(F32, ROWS, EMB),
         inv=two(F32, ROWS, EMB),
         plane=two(BF16, nz, ny, ROWS, EMB),
@@ -63,13 +64,11 @@
         from_core=two(F32, nx, ROWS, EMB),
         core_sum=two(F32, nx, ROWS, EMB),
         from_x=two(F32, nx - 1, ROWS, EMB),
-        dw=two(F32, nk, 3, ROWS, WIDE),
-        from_pair=two(F32, 3, ROWS, WIDE),
-        pair_sum=two(F32, 3, ROWS, WIDE),
-        ra=six(lambda a, b, c: (a - 1, ROWS // a)),
-        sa=six(lambda a, b, c: (ROWS // a,)),
-        rb=six(lambda a, b, c: (b - 1, ROWS // a // b)),
-        cx=six(lambda a, b, c: (c, ROWS // a // b)),
+        dw=vm(F32, 3, 2, ROWS, WIDE),
+        ra=each(lambda a, b, c: (a - 1, 2, ROWS // a)),
+        sa=each(lambda a, b, c: (2, ROWS // a)),
+        rb=each(lambda a, b, c: (b - 1, 2, ROWS // a // b)),
+        cx=each(lambda a, b, c: (c, 2, ROWS // a // b)),
         meta_plane=vm(F32, nz, ny, 8, ROWS),
         meta_small=vm(F32, nk, nx, 8, ROWS),
         lqc_plane=vm(F32, nz, ny, ROWS, ROWS),
@@ -95,7 +94,6 @@
         pos=vm(F32, 1, ROWS),
         send_sem=pltpu.SemaphoreType.DMA((N_REMOTE,)),
         recv_sem=pltpu.SemaphoreType.DMA((N_REMOTE,)),
-        load_sem=pltpu.SemaphoreType.DMA((8,)),
     )
 
 
@@ -195,19 +193,6 @@
             started[drained[0]].wait_send()
             drained[0] += 1
 
-    loads = []
-
-    def load(src, dst):
-        copy = pltpu.make_async_copy(src, dst, s.load_sem.at[len(loads)])
-        copy.start()
-        loads.append(copy)
-        return copy
-
-    load_x, load_w = {}, {}
-    for t in (1, 0):
-        load_x[t] = load(x_in[t], s.xf[t])
-        load_w[t] = [load(w_in[t][i], s.wf[t][i]) for i in range(3)]
-
     barrier = pltpu.get_barrier_semaphore()
     greet = [at_peer(ax, r) for ax in (AZ, AY, AX, AK) for r in range(1, size[ax])]
     greet += [me + (wrap(AK, rk) - k) + (wrap(AX, rx) - x) * nk for rk in range(1, nk) for rx in range(1, nx)]
@@ -223,11 +208,9 @@
     s.meta_small[k, x] = meta
 
     def forward(t):
-        load_x[t].wait()
-        xb = s.xf[t][...].astype(BF16)
+        xb = x_in[t][...].astype(BF16)
         for i in range(3):
-            load_w[t][i].wait()
-            s.wh[t][i][...] = s.wf[t][i][...].astype(BF16)
+            s.wh[t][i][...] = w_in[t][i][...].astype(BF16)
         act = jnp.maximum(mm(xb, s.wh[t][0][...]), 0.0).astype(BF16)
         s.h1[t][...] = act
         act = jnp.maximum(mm(act, s.wh[t][1][...]), 0.0).astype(BF16)
@@ -258,24 +241,23 @@
 
     forward(1)
     pl.semaphore_wait(barrier, len(greet))
+    meta_y = share(AY, s.meta_plane.at[z, y])
+    meta_x = share(AX, s.meta_small.at[k, x])
     v_first = plane_first(1)
     v_small = share(AX, s.small[1].at[k, x])
-    meta_y = share(AY, s.meta_plane.at[z, y])
-    meta_x = share(AX, s.meta_small.at[k, x])
     forward(0)
     u_small = share(AX, s.small[0].at[k, x])
     u_first = plane_first(0)
-    v_second = plane_second(1, v_first)
     meta_y.recv()
     meta_z = share(AZ, s.meta_plane.at[z])
     meta_x.recv()
     meta_k = share(AK, s.meta_small.at[k])
+    v_second = plane_second(1, v_first)
     u_small.recv()
     u_small_k = share(AK, s.small[0].at[k])
     u_second = plane_second(0, u_first)
     v_small.recv()
     v_small_k = share(AK, s.small[1].at[k])
-    gathers = len(started)
 
     def columns(ref, lq_out, id_out, id_row, count, nested):
         flat = ref[...].reshape(count * 8, ROWS)
@@ -300,9 +282,13 @@
         return value.astype(F32).T.astype(BF16)
 
     for t in (0, 1):
-        s.xt[t][...] = s.xf[t][...].T.astype(BF16)
-        s.h1t[t][...] = transposed(s.h1[t][...])
-        s.h2t[t][...] = transposed(s.h2[t][...])
+        s.xt[t, k] = x_in[t][...].T.astype(BF16)
+        s.h1t[t, k] = transposed(s.h1[t][...])
+        s.h2t[t, k] = transposed(s.h2[t][...])
+    saved = Exchange([(i, None, at_peer(AK, 1)) for i in range(3)])
+    for i, ref in enumerate((s.xt, s.h1t, s.h2t)):
+        saved.post(i, ref.at[1 - k, k], ref.at[1 - k, k])
+    saved_end = len(started)
 
     v_own = s.small[1][k, x]
     u_own = s.small[0][k, x]
@@ -444,7 +430,7 @@
     lax.fori_loop(n_chunk // 2, n_chunk, user_chunk, 0)
     s.parts[0][own_block] = s.parts[0][own_block] + mm(v_own, s.own_diag[...], C00)
     du_x = to_x(0, du_core)
-    drain(gathers)
+    drain(saved_end)
     ml_plane.recv()
     loss_row = jnp.zeros((1, ROWS), F32)
     for iz in range(nz):
@@ -490,136 +476,153 @@
     def backward(t, grad_unit):
         unit = s.unit[t][...]
         grad_raw = s.inv[t][...] * (grad_unit - unit * jnp.sum(unit * grad_unit, axis=1, keepdims=True))
-        grad_half = grad_raw.astype(BF16)
-        dw = s.dw[t]
-        back = mm(grad_half, s.wh[t][2][...], C11)
+        grad_three = grad_raw.astype(BF16)
+        s.g3[t, k] = grad_three
+        back = mm(grad_three, s.wh[t][2][...], C11)
         grad_two = jnp.where(s.h2[t][...] > 0, back, 0.0).astype(BF16)
+        s.g2[t, k] = grad_two
         back = mm(grad_two, s.wh[t][1][...], C11)
-        grad_one = jnp.where(s.h1[t][...] > 0, back, 0.0).astype(BF16)
-        third = mm(s.h2t[t][...], grad_half)
-        for i in range(3):
-            dw[0, 2, :, i * EMB:(i + 1) * EMB] = third[i * ROWS:(i + 1) * ROWS]
-        second = mm(s.h1t[t][...], grad_two)
-        for i in range(3):
-            dw[1, i] = second[i * ROWS:(i + 1) * ROWS]
-        first = mm(s.xt[t][...], grad_one)
-        for i in range(2):
-            dw[0, i] = first[i * ROWS:(i + 1) * ROWS]
+        s.g1[t, k] = jnp.where(s.h1[t][...] > 0, back, 0.0).astype(BF16)
 
     axes = ((AX, AY, AZ), (AY, AZ, AX), (AZ, AX, AY))
-
-    class WeightSum:
-        def __init__(self, t):
-            self.t = t
-
-        def rows(self, q, deep):
-            a, b, _ = axes[q]
-            high = ROWS // size[a]
-            if not deep:
-                return pl.ds(pl.multiple_of(co[a] * high, high), high)
-            step = high // size[b]
-            return pl.ds(pl.multiple_of(co[a] * high + co[b] * step, step), step)
-
-        def pair(self):
-            ref, into = s.dw[self.t], s.from_pair[self.t]
-            self.open = [along(AK).send(lambda r, d: ref.at[1 - k], lambda r, d: into)]
-
-        def close(self):
-            for exchange in self.open:
-                exchange.recv()
-
-        def scatter_one(self):
-            self.close()
-            self.open = []
-            for q in range(3):
-                total = s.pair_sum[self.t]
-                total[q] = s.dw[self.t][k, q] + s.from_pair[self.t][q]
-                high = ROWS // size[axes[q][0]]
-                self.open.append(along(axes[q][0]).send(
-                    lambda r, d, q=q, high=high: total.at[q, pl.ds(pl.multiple_of(d * high, high), high)],
-                    lambda r, d, q=q: s.ra[self.t][q].at[r - 1]))
-
-        def scatter_two(self):
-            done, self.open = self.open, []
-            for q in range(3):
-                done[q].recv()
-                value = s.pair_sum[self.t][q, self.rows(q, False)]
-                for r in range(size[axes[q][0]] - 1):
-                    value = value + s.ra[self.t][q][r]
-                s.sa[self.t][q][...] = value
-                step = ROWS // size[axes[q][0]] // size[axes[q][1]]
-                self.open.append(along(axes[q][1]).send(
-                    lambda r, d, q=q, step=step: s.sa[self.t][q].at[pl.ds(pl.multiple_of(d * step, step), step)],
-                    lambda r, d, q=q: s.rb[self.t][q].at[r - 1]))
-
-        def exchange_three(self):
-            done, self.open = self.open, []
-            for q in range(3):
-                done[q].recv()
-                a, b, c = axes[q]
-                step = ROWS // size[a] // size[b]
-                value = s.sa[self.t][q][pl.ds(pl.multiple_of(co[b] * step, step), step)]
-                for r in range(size[b] - 1):
-                    value = value + s.rb[self.t][q][r]
-                s.cx[self.t][q][co[c]] = value
-                self.open.append(share(c, s.cx[self.t][q].at[co[c]]))
-
-        def gather_two(self):
-            done, self.open = self.open, []
-            for q in range(3):
-                done[q].recv()
-                value = s.cx[self.t][q][0]
-                for r in range(1, size[axes[q][2]]):
-                    value = value + s.cx[self.t][q][r]
-                out_ref[k, self.t, q, self.rows(q, True)] = value
-                self.open.append(share(axes[q][1], out_ref.at[k, self.t, q, self.rows(q, True)]))
-
-        def gather_one(self):
-            done, self.open = self.open, []
-            for q in range(3):
-                done[q].recv()
-                self.open.append(share(axes[q][0], out_ref.at[k, self.t, q, self.rows(q, False)]))
-
-        def hand_over(self):
-            done, self.open = self.open, []
-            for q in range(3):
-                done[q].recv()
-                self.open.append(share(AK, out_ref.at[k, self.t, q]))
-
-    user, item = WeightSum(0), WeightSum(1)
-    backward(0, summed(0, du_x).T)
-    user.pair()
-    user.scatter_one()
-    backward(1, summed(1, dv_x))
-    item.pair()
+    own_rows = [[None, None] for _ in axes]
+    for q, (first, second, _) in enumerate(axes):
+        high = ROWS // size[first]
+        step = high // size[second]
+        own_rows[q][0] = pl.ds(pl.multiple_of(co[first] * high, high), high)
+        own_rows[q][1] = pl.ds(pl.multiple_of(co[first] * high + co[second] * step, step), step)
+    scatter_a = [along(axes[q][0]) for q in range(3)]
+
+    def pair_copy(t, i):
+        ref = (s.g3, s.g2, s.g1)[i].at[t, 1 - t]
+        index = grad_pair.base + 3 * t + i
+        return pltpu.make_async_remote_copy(
+            src_ref=ref, dst_ref=ref, send_sem=s.send_sem.at[index], recv_sem=s.recv_sem.at[index],
+            device_id=(grad_pair.peers[0][2],), device_id_type=MESH)
+
+    grad_pair = Exchange([(i, None, at_peer(AK, 1)) for i in range(6)])
+
+    def hand_grads(t):
+        @pl.when(k != t)
+        def _():
+            for i in range(3):
+                pair_copy(t, i).start()
+
+    def weight_grads(t):
+        @pl.when(k == t)
+        def _():
+            def rows(ref, depth):
+                return jnp.concatenate([ref[t, i] for i in range(nk)], axis=1)
+
+            pair_copy(t, 0).wait_recv()
+            third = mm(rows(s.h2t, WIDE), s.g3[t].reshape(nk * ROWS, EMB))
+            for i in range(3):
+                s.dw[2, 1, :, i * EMB:(i + 1) * EMB] = third[i * ROWS:(i + 1) * ROWS]
+            pair_copy(t, 1).wait_recv()
+            second = mm(rows(s.h1t, WIDE), s.g2[t].reshape(nk * ROWS, WIDE))
+            s.dw[1, 0] = second[:ROWS]
+            s.dw[1, 1] = second[ROWS:2 * ROWS]
+            s.dw[2, 0] = second[2 * ROWS:]
+            start_scatter(2)
+            start_scatter(1)
+            pair_copy(t, 2).wait_recv()
+            first = mm(rows(s.xt, IN_WIDTH), s.g1[t].reshape(nk * ROWS, WIDE))
+            s.dw[0, 0] = first[:ROWS]
+            s.dw[0, 1] = first[ROWS:]
+            start_scatter(0)
+
+    def scatter_copy(q, i):
+        high = ROWS // size[axes[q][0]]
+        r, dest, dev = scatter_a[q].peers[i]
+        index = scatter_a[q].base + i
+        return pltpu.make_async_remote_copy(
+            src_ref=s.dw.at[q, :, pl.ds(pl.multiple_of(dest * high, high), high)], dst_ref=s.ra[q].at[r - 1],
+            send_sem=s.send_sem.at[index], recv_sem=s.recv_sem.at[index],
+            device_id=(dev,), device_id_type=MESH)
+
+    def start_scatter(q):
+        for i in range(len(scatter_a[q].peers)):
+            scatter_copy(q, i).start()
+
+    grad_user = summed(0, du_x).T
+    backward(0, grad_user)
+    hand_grads(0)
+    saved.recv()
+    weight_grads(0)
     drain(middle)
-    user.scatter_two()
-    item.scatter_one()
-    early = len(started)
-    user.exchange_three()
-    item.scatter_two()
-    drain(early)
-    early = len(started)
-    user.gather_two()
-    item.exchange_three()
-    drain(early)
-    early = len(started)
-    user.gather_one()
-    item.gather_two()
-    drain(early)
-    early = len(started)
-    user.hand_over()
-    item.gather_one()
-    drain(early)
+    grad_item = summed(1, dv_x)
+    backward(1, grad_item)
+    hand_grads(1)
+    weight_grads(1)
+    order_q = (2, 1, 0)
+    scatter_b = {}
+    for q in order_q:
+        for i in range(len(scatter_a[q].peers)):
+            scatter_copy(q, i).wait_recv()
+        first, second, _ = axes[q]
+        value = s.dw[q, :, own_rows[q][0]]
+        for r in range(size[first] - 1):
+            value = value + s.ra[q][r]
+        s.sa[q][...] = value
+        step = ROWS // size[first] // size[second]
+        scatter_b[q] = along(second).send(
+            lambda r, d, q=q, step=step: s.sa[q].at[:, pl.ds(pl.multiple_of(d * step, step), step)],
+            lambda r, d, q=q: s.rb[q].at[r - 1])
+    for q in order_q:
+        for i in range(len(scatter_a[q].peers)):
+            scatter_copy(q, i).wait_send()
+    for t in range(2):
+        @pl.when(k != t)
+        def _():
+            for i in range(3):
+                pair_copy(t, i).wait_send()
+    second_end = len(started)
+    exchange_c = {}
+    for q in order_q:
+        scatter_b[q].recv()
+        first, second, third = axes[q]
+        step = ROWS // size[first] // size[second]
+        value = s.sa[q][:, pl.ds(pl.multiple_of(co[second] * step, step), step)]
+        for r in range(size[second] - 1):
+            value = value + s.rb[q][r]
+        s.cx[q][co[third]] = value
+        exchange_c[q] = share(third, s.cx[q].at[co[third]])
+    drain(second_end)
+    third_end = len(started)
+    gather_b = {}
+    for q in order_q:
+        exchange_c[q].recv()
+        value = s.cx[q][0]
+        for r in range(1, size[axes[q][2]]):
+            value = value + s.cx[q][r]
+        out_ref[k, q, :, own_rows[q][1]] = value
+        gather_b[q] = share(axes[q][1], out_ref.at[k, q, :, own_rows[q][1]])
+    drain(third_end)
     loss_x.recv()
     loss_total = jnp.zeros((8, ROWS), F32)
     for ik in range(nk):
         for ix in range(nx):
             loss_total = loss_total + s.lx[ik, ix]
     loss_ref[...] = loss_total
-    user.close()
-    item.hand_over()
-    item.close()
+    fourth_end = len(started)
+    gather_a = {}
+    handed = []
+    for q in order_q:
+        gather_b[q].recv()
+        gather_a[q] = share(axes[q][0], out_ref.at[k, q, :, own_rows[q][0]])
+    for q in order_q:
+        handed.append(share(AK, out_ref.at[k, q, :, own_rows[q][0]]))
+    drain(fourth_end)
+    for i in range(max(size) - 1):
+        for q in order_q:
+            first = axes[q][0]
+            high = ROWS // size[first]
+            r = gather_a[q].peers[i][0]
+            gather_a[q].copies[i].wait_recv()
+            source = lax.rem(co[first] - r + size[first], size[first])
+            handed.append(share(AK, out_ref.at[k, q, :, pl.ds(pl.multiple_of(source * high, high), high)]))
+    for exchange in handed:
+        exchange.recv()
     drain(len(started))
 
 
@@ -628,10 +631,10 @@
     for t in range(2):
         one, two, three = outs[3 * t:3 * t + 3]
         for i in range(2):
-            one[i * ROWS:(i + 1) * ROWS] = res_ref[0, t, i]
+            one[i * ROWS:(i + 1) * ROWS] = res_ref[t, 0, i]
         for i in range(3):
-            two[i * ROWS:(i + 1) * ROWS] = res_ref[1, t, i]
-            three[i * ROWS:(i + 1) * ROWS] = res_ref[0, t, 2, :, i * EMB:(i + 1) * EMB]
+            two[i * ROWS:(i + 1) * ROWS] = res_ref[t, 1 + i // 2, i % 2]
+            three[i * ROWS:(i + 1) * ROWS] = res_ref[t, 2, 1, :, i * EMB:(i + 1) * EMB]
 
 
 def solution(mesh):
@@ -639,16 +642,15 @@
     grid = GRIDS[devices]
     scratch, tree = jax.tree.flatten(scratch_table(*grid))
     vmem = pl.BlockSpec(memory_space=pltpu.VMEM)
-    hbm = pl.BlockSpec(memory_space=pltpu.HBM)
 
     def device_step(user_x, item_x, item_id, log_q, user_w1, user_w2, user_w3, item_w1, item_w2, item_w3):
         res, loss_rows = pl.pallas_call(
             functools.partial(step_kernel, grid, tree),
-            out_shape=(jax.ShapeDtypeStruct((grid[3], 2, 3, ROWS, WIDE), F32), jax.ShapeDtypeStruct((8, ROWS), F32)),
-            in_specs=[hbm, hbm, vmem, vmem] + [hbm] * 6,
+            out_shape=(jax.ShapeDtypeStruct((2, 3, 2, ROWS, WIDE), F32), jax.ShapeDtypeStruct((8, ROWS), F32)),
+            in_specs=[vmem] * 10,
             out_specs=(vmem, vmem),
             scratch_shapes=scratch,
-            compiler_params=pltpu.CompilerParams(collective_id=0, has_side_effects=True, vmem_limit_bytes=60 * 1024 * 1024),
+            compiler_params=pltpu.CompilerParams(collective_id=0, has_side_effects=True, vmem_limit_bytes=40 * 1024 * 1024),
             name='train_step',
         )(user_x, item_x, log_q.reshape(1, ROWS), item_id.reshape(1, ROWS), user_w1, user_w2, user_w3, item_w1, item_w2, item_w3)
         shapes = [(IN_WIDTH, WIDE), (WIDE, WIDE), (WIDE, EMB)] * 2
@@ -657,6 +659,7 @@
             out_shape=[jax.ShapeDtypeStruct((1, 1), F32)] + [jax.ShapeDtypeStruct(shape, F32) for shape in shapes],
             in_specs=[vmem, vmem],
             out_specs=[vmem] * 7,
+            compiler_params=pltpu.CompilerParams(vmem_limit_bytes=12 * 1024 * 1024),
             name='finish',
         )(res, loss_rows)
         return (outs[0].reshape(()),) + tuple(outs[1:])

time: 75.5 us -> 76.2 us (level)
  local copies, waits for them, and re-layouts: 0 us -> 9.08 us
  Pallas kernels: 74.7 us -> 66.1 us
    unnamed x0 -> x20, local copies, waits for them, and re-layouts: none -> 9.08 us
    pallas_call x1, Pallas kernels: 71.6 us -> 64.6 us  [device_step(): pl.pallas_call(functools.partial(step_kernel, grid, tree), out_shape=(jax...]
    pallas_call x1, Pallas kernels: 3.09 us -> 1.42 us  [device_step(): pl.pallas_call(functools.partial(finish_kernel, float(devices * ROWS)), o...]
where the time goes in v3:
time: 76.2 us; the launch traced here: 75.8 us
  Pallas kernels  66.1 us (87%)
  local copies, waits for them, and re-layouts  9.08 us (12%)
    pallas_call x1, Pallas kernels, device_step(): pl.pallas_call(functools.partial(step_kernel, grid, tree), out_shape=(jax...  64.6 us
    unnamed x20, local copies, waits for them, and re-layouts  9.08 us

profile of v3, /device:TPU:1, one launch (start us, length us, event | category | flops | bytes accessed | tf_op | source)
XLA Modules:
  0.0 75.8 jit_solution(6033774799464998492)
XLA Ops:
  0.6 0.0 copy-start
  0.6 1.1 %copy-done = f32[384,384]{1,0:T(8,128)S(1)} copy-done((f32[384,384]{1,0:T(8,128)S(1)}, f32[384,384]{1,0:T(8,128)}, u32[]{:S(2)}) %copy-start) | copy-done | bytes 589848
  1.7 0.0 copy-start.1
  1.7 1.1 %copy-done.1 = f32[384,384]{1,0:T(8,128)S(1)} copy-done((f32[384,384]{1,0:T(8,128)S(1)}, f32[384,384]{1,0:T(8,128)}, u32[]{:S(2)}) %copy-start.1) | copy-done | bytes 589848
  2.8 0.0 copy-start.2
  2.8 1.0 %copy-done.2 = f32[256,384]{1,0:T(8,128)S(1)} copy-done((f32[256,384]{1,0:T(8,128)S(1)}, f32[256,384]{1,0:T(8,128)}, u32[]{:S(2)}) %copy-start.2) | copy-done | bytes 393240
  3.8 0.0 copy-start.3
  3.8 1.0 %copy-done.3 = f32[256,384]{1,0:T(8,128)S(1)} copy-done((f32[256,384]{1,0:T(8,128)S(1)}, f32[256,384]{1,0:T(8,128)}, u32[]{:S(2)}) %copy-start.3) | copy-done | bytes 393240
  4.8 0.0 copy-start.4
  4.8 0.9 %copy-done.4 = f32[384,128]{1,0:T(8,128)S(1)} copy-done((f32[384,128]{1,0:T(8,128)S(1)}, f32[384,128]{1,0:T(8,128)}, u32[]{:S(2)}) %copy-start.4) | copy-done | bytes 196632
  5.7 0.0 copy-start.5
  5.7 0.9 %copy-done.5 = f32[384,128]{1,0:T(8,128)S(1)} copy-done((f32[384,128]{1,0:T(8,128)S(1)}, f32[384,128]{1,0:T(8,128)}, u32[]{:S(2)}) %copy-start.5) | copy-done | bytes 196632
  6.6 0.0 copy-start.6
  6.6 0.9 %copy-done.6 = f32[128,256]{1,0:T(8,128)S(1)} copy-done((f32[128,256]{1,0:T(8,128)S(1)}, f32[128,256]{1,0:T(8,128)}, u32[]{:S(2)}) %copy-start.6) | copy-done | bytes 131096
  7.5 0.0 copy-start.7
  7.5 0.9 %copy-done.7 = f32[128,256]{1,0:T(8,128)S(1)} copy-done((f32[128,256]{1,0:T(8,128)S(1)}, f32[128,256]{1,0:T(8,128)}, u32[]{:S(2)}) %copy-start.7) | copy-done | bytes 131096
  8.4 0.0 copy-start.8
  8.4 0.7 copy-done.8
  9.1 0.0 copy-start.9
  9.1 0.7 copy-done.9
  9.7 64.6 %train_step.1 = (f32[2,3,2,128,384]{4,3,2,1,0:T(8,128)S(1)}, f32[8,128]{1,0:T(8,128)S(1)}) custom-call(f32[128,256]{1,0:T(8,128)S(1)} %copy-done.6, f32[128,256]{1,0:T(8,128)S(1)} %copy-done.7, f32[1,128]{1,0:T(1,128)S(1)} %bitcast.3, s32[1,128]{1,0:T(1,128)S(1)} %bitcast.4, f32[256,384]{1,0:T(8,128)S(1)} %copy-done.2, f32[384,384]{1,0:T(8,128)S(1)} %copy-done, ...), custom_call_target="tpu_custom_call" | custom-call | tf_op jit(solution)/shard_map/train_step/pallas_call | solution.py:647
  74.4 1.4 %finish.1 = (f32[1,1]{1,0:T(1,128)}, f32[256,384]{1,0:T(8,128)}, f32[384,384]{1,0:T(8,128)}, f32[384,128]{1,0:T(8,128)}, f32[256,384]{1,0:T(8,128)}, /*index=5*/f32[384,384]{1,0:T(8,128)}, f32[384,128]{1,0:T(8,128)}) custom-call(f32[2,3,2,128,384]{4,3,2,1,0:T(8,128)S(1)} %get-tuple-element.16.res_ref, f32[8,128]{1,0:T(8,128)S(1)} %get-tuple-element.17.loss_in), custom_call_target="tpu_custom_call" | custom-call | tf_op jit(solution)/shard_map/finish/pallas_call | solution.py:657
Async XLA Ops:
  0.6 1.1 %copy-start = (f32[384,384]{1,0:T(8,128)S(1)}, f32[384,384]{1,0:T(8,128)}, u32[]{:S(2)}) copy-start(f32[384,384]{1,0:T(8,128)} %refs_5_.1) | copy-start | bytes 1769476
  1.7 1.1 %copy-start.1 = (f32[384,384]{1,0:T(8,128)S(1)}, f32[384,384]{1,0:T(8,128)}, u32[]{:S(2)}) copy-start(f32[384,384]{1,0:T(8,128)} %refs_8_.1) | copy-start | bytes 1769476
  2.8 1.0 %copy-start.2 = (f32[256,384]{1,0:T(8,128)S(1)}, f32[256,384]{1,0:T(8,128)}, u32[]{:S(2)}) copy-start(f32[256,384]{1,0:T(8,128)} %refs_4_.1) | copy-start | bytes 1179652
  3.8 1.0 %copy-start.3 = (f32[256,384]{1,0:T(8,128)S(1)}, f32[256,384]{1,0:T(8,128)}, u32[]{:S(2)}) copy-start(f32[256,384]{1,0:T(8,128)} %refs_7_.1) | copy-start | bytes 1179652
  4.8 0.9 %copy-start.4 = (f32[384,128]{1,0:T(8,128)S(1)}, f32[384,128]{1,0:T(8,128)}, u32[]{:S(2)}) copy-start(f32[384,128]{1,0:T(8,128)} %refs_6_.1) | copy-start | bytes 589828
  5.7 0.9 %copy-start.5 = (f32[384,128]{1,0:T(8,128)S(1)}, f32[384,128]{1,0:T(8,128)}, u32[]{:S(2)}) copy-start(f32[384,128]{1,0:T(8,128)} %refs_9_.1) | copy-start | bytes 589828
  6.6 0.9 %copy-start.6 = (f32[128,256]{1,0:T(8,128)S(1)}, f32[128,256]{1,0:T(8,128)}, u32[]{:S(2)}) copy-start(f32[128,256]{1,0:T(8,128)} %refs_0_.1) | copy-start | bytes 393220
  7.5 0.9 %copy-start.7 = (f32[128,256]{1,0:T(8,128)S(1)}, f32[128,256]{1,0:T(8,128)}, u32[]{:S(2)}) copy-start(f32[128,256]{1,0:T(8,128)} %refs_1_.1) | copy-start | bytes 393220
  8.4 0.7 copy-start.8
  9.1 0.7 copy-start.9

commit v4 on v3

--- a/solution.py
+++ b/solution.py
@@ -48,6 +48,10 @@
 
     return dict(
         wh=[[vm(BF16, IN_WIDTH, WIDE), vm(BF16, WIDE, WIDE), vm(BF16, WIDE, EMB)] for _ in range(2)],
+        xf=two(F32, ROWS, IN_WIDTH),
+        wf=[[vm(F32, IN_WIDTH, WIDE), vm(F32, WIDE, WIDE), vm(F32, WIDE, EMB)] for _ in range(2)],
+        lq=vm(F32, 1, ROWS),
+        ids=vm(jnp.int32, 1, ROWS),
         h1=two(BF16, ROWS, WIDE),
         h2=two(BF16, ROWS, WIDE),
         xt=vm(BF16, 2, nk, IN_WIDTH, ROWS),
@@ -86,6 +90,7 @@
         plane_t=vm(BF16, EMB, n_wide),
         grad_tile=vm(BF16, n_wide, 256),
         scores=vm(F32, n_small // 2, 256, n_wide),
+        chunk_max=vm(F32, n_small // 2, 1, n_wide),
         row_max=vm(F32, 1, longest),
         row_inv=vm(F32, 1, longest),
         ml=vm(F32, nz, ny, 8, ROWS),
@@ -94,6 +99,7 @@
         pos=vm(F32, 1, ROWS),
         send_sem=pltpu.SemaphoreType.DMA((N_REMOTE,)),
         recv_sem=pltpu.SemaphoreType.DMA((N_REMOTE,)),
+        load_sem=pltpu.SemaphoreType.DMA((10,)),
     )
 
 
@@ -193,6 +199,21 @@
             started[drained[0]].wait_send()
             drained[0] += 1
 
+    loads = []
+
+    def load(src, dst):
+        copy = pltpu.make_async_copy(src, dst, s.load_sem.at[len(loads)])
+        copy.start()
+        loads.append(copy)
+        return copy
+
+    load_x, load_w = {}, {}
+    for t in (1, 0):
+        load_x[t] = load(x_in[t], s.xf[t])
+        load_w[t] = [load(w_in[t][i], s.wf[t][i]) for i in range(3)]
+        if t:
+            load_meta = load(lq_in, s.lq), load(id_in, s.ids)
+
     barrier = pltpu.get_barrier_semaphore()
     greet = [at_peer(ax, r) for ax in (AZ, AY, AX, AK) for r in range(1, size[ax])]
     greet += [me + (wrap(AK, rk) - k) + (wrap(AX, rx) - x) * nk for rk in range(1, nk) for rx in range(1, nx)]
@@ -200,17 +221,12 @@
     for dev in greet:
         pl.semaphore_signal(barrier, inc=1, device_id=(dev,), device_id_type=MESH)
 
-    ids = id_in[...]
-    zero_row = jnp.zeros((1, ROWS), F32)
-    meta = jnp.concatenate([lq_in[...], lax.shift_right_logical(ids, 16).astype(F32),
-                            lax.bitwise_and(ids, 65535).astype(F32)] + [zero_row] * 5, axis=0)
-    s.meta_plane[z, y] = meta
-    s.meta_small[k, x] = meta
-
     def forward(t):
-        xb = x_in[t][...].astype(BF16)
+        load_x[t].wait()
+        xb = s.xf[t][...].astype(BF16)
         for i in range(3):
-            s.wh[t][i][...] = w_in[t][i][...].astype(BF16)
+            load_w[t][i].wait()
+            s.wh[t][i][...] = s.wf[t][i][...].astype(BF16)
         act = jnp.maximum(mm(xb, s.wh[t][0][...]), 0.0).astype(BF16)
         s.h1[t][...] = act
         act = jnp.maximum(mm(act, s.wh[t][1][...]), 0.0).astype(BF16)
@@ -240,6 +256,14 @@
         return a, b
 
     forward(1)
+    for copy in load_meta:
+        copy.wait()
+    ids = s.ids[...]
+    zero_row = jnp.zeros((1, ROWS), F32)
+    meta = jnp.concatenate([s.lq[...], lax.shift_right_logical(ids, 16).astype(F32),
+                            lax.bitwise_and(ids, 65535).astype(F32)] + [zero_row] * 5, axis=0)
+    s.meta_plane[z, y] = meta
+    s.meta_small[k, x] = meta
     pl.semaphore_wait(barrier, len(greet))
     meta_y = share(AY, s.meta_plane.at[z, y])
     meta_x = share(AX, s.meta_small.at[k, x])
@@ -253,12 +277,6 @@
     meta_x.recv()
     meta_k = share(AK, s.meta_small.at[k])
     v_second = plane_second(1, v_first)
-    u_small.recv()
-    u_small_k = share(AK, s.small[0].at[k])
-    u_second = plane_second(0, u_first)
-    v_small.recv()
-    v_small_k = share(AK, s.small[1].at[k])
-
     def columns(ref, lq_out, id_out, id_row, count, nested):
         flat = ref[...].reshape(count * 8, ROWS)
         if count * 8 < ROWS:
@@ -281,8 +299,14 @@
     def transposed(value):
         return value.astype(F32).T.astype(BF16)
 
+    u_small.recv()
+    u_small_k = share(AK, s.small[0].at[k])
+    u_second = plane_second(0, u_first)
+    v_small.recv()
+    v_small_k = share(AK, s.small[1].at[k])
+
     for t in (0, 1):
-        s.xt[t, k] = x_in[t][...].T.astype(BF16)
+        s.xt[t, k] = s.xf[t][...].T.astype(BF16)
         s.h1t[t, k] = transposed(s.h1[t][...])
         s.h2t[t, k] = transposed(s.h2[t][...])
     saved = Exchange([(i, None, at_peer(AK, 1)) for i in range(3)])
@@ -369,10 +393,13 @@
             lanes = slice(n * 256, (n + 1) * 256)
             queries = s.plane[0][2 * n // ny, pl.ds(2 * n % ny, 2)].reshape(256, EMB)
             score = mm(items, queries, C11) * INV_TEMP - lq_wide
-            s.scores[chunk, :, lanes] = jnp.where(id_wide == s.idr_plane[:, lanes], -jnp.inf, score)
+            score = jnp.where(id_wide == s.idr_plane[:, lanes], -jnp.inf, score)
+            peak = jnp.maximum(jnp.max(score, axis=0, keepdims=True), NEG)
+            s.scores[chunk, :, lanes] = jnp.exp(score - peak)
+            s.chunk_max[chunk, :, lanes] = peak
         return carry
 
-    lax.fori_loop(0, n_chunk, wide_tile, 0)
+    lax.fori_loop(0, 3 * n_chunk // 4, wide_tile, 0)
 
     stats.recv()
     every = s.stats[...].reshape(n_small, 2 * n_small, ROWS)
@@ -389,7 +416,7 @@
     own_max = s.stat_all[pl.ds(own_block, 1)]
     own_sum = s.stat_all[pl.ds(n_small + own_block, 1)]
     s.ml[z, y] = jnp.concatenate([own_max, own_sum, pos] + [zero_row] * 5, axis=0)
-    ml_ref = s.ml.at[z, y]
+    ml_ref = s.ml.at[z, y, pl.ds(0, 3)]
     ml_plane = plane_group().send(lambda r, d: ml_ref, lambda r, d: ml_ref)
     own_grad = (jnp.exp(pos - own_max) / own_sum - 1.0) / batch
     s.own_diag[...] = jnp.where(eye, jnp.broadcast_to(own_grad, (ROWS, ROWS)), 0.0).astype(BF16)
@@ -431,6 +458,7 @@
     s.parts[0][own_block] = s.parts[0][own_block] + mm(v_own, s.own_diag[...], C00)
     du_x = to_x(0, du_core)
     drain(saved_end)
+    lax.fori_loop(3 * n_chunk // 4, n_chunk, wide_tile, 0)
     ml_plane.recv()
     loss_row = jnp.zeros((1, ROWS), F32)
     for iz in range(nz):
@@ -449,8 +477,8 @@
         grads = []
         for n in range(n_wide_tile):
             lanes = slice(n * 256, (n + 1) * 256)
-            grads.append((jnp.exp(s.scores[chunk, :, lanes] - s.row_max[:, lanes])
-                          * s.row_inv[:, lanes]).astype(BF16))
+            factor = jnp.exp(s.chunk_max[chunk, :, lanes] - s.row_max[:, lanes]) * s.row_inv[:, lanes]
+            grads.append((s.scores[chunk, :, lanes] * factor).astype(BF16))
         total = mm(jnp.concatenate(grads, axis=1), s.plane[0][...].reshape(n_wide, EMB))
         for i, r in enumerate(stages[stage]):
             s.parts[1][side * nx + wrap(AX, r)] = total[i * ROWS:(i + 1) * ROWS]
@@ -642,17 +670,20 @@
     grid = GRIDS[devices]
     scratch, tree = jax.tree.flatten(scratch_table(*grid))
     vmem = pl.BlockSpec(memory_space=pltpu.VMEM)
+    hbm = pl.BlockSpec(memory_space=pltpu.HBM)
 
     def device_step(user_x, item_x, item_id, log_q, user_w1, user_w2, user_w3, item_w1, item_w2, item_w3):
+        operands = (user_x, item_x, log_q.reshape(1, ROWS), item_id.reshape(1, ROWS),
+                    user_w1, user_w2, user_w3, item_w1, item_w2, item_w3)
         res, loss_rows = pl.pallas_call(
             functools.partial(step_kernel, grid, tree),
             out_shape=(jax.ShapeDtypeStruct((2, 3, 2, ROWS, WIDE), F32), jax.ShapeDtypeStruct((8, ROWS), F32)),
-            in_specs=[vmem] * 10,
+            in_specs=[hbm] * 10,
             out_specs=(vmem, vmem),
             scratch_shapes=scratch,
             compiler_params=pltpu.CompilerParams(collective_id=0, has_side_effects=True, vmem_limit_bytes=40 * 1024 * 1024),
             name='train_step',
-        )(user_x, item_x, log_q.reshape(1, ROWS), item_id.reshape(1, ROWS), user_w1, user_w2, user_w3, item_w1, item_w2, item_w3)
+        )(*[pltpu.with_memory_space_constraint(value, pltpu.HBM) for value in operands])
         shapes = [(IN_WIDTH, WIDE), (WIDE, WIDE), (WIDE, EMB)] * 2
         outs = pl.pallas_call(
             functools.partial(finish_kernel, float(devices * ROWS)),

time: 76.2 us -> 67 us (0.88)
  local copies, waits for them, and re-layouts: 9.08 us -> 0 us
    unnamed x20 -> x0, local copies, waits for them, and re-layouts: 9.08 us -> none
where the time goes in v4:
time: 67 us; the launch traced here: 66.8 us
  Pallas kernels  66.2 us (99%)
    pallas_call x1, Pallas kernels, device_step(): pl.pallas_call(functools.partial(step_kernel, grid, tree), out_shape=(jax...  64.8 us
    pallas_call x1, Pallas kernels, device_step(): pl.pallas_call(functools.partial(finish_kernel, float(devices * ROWS)), o...  1.42 us

profile of v4, /device:TPU:1, one launch (start us, length us, event | category | flops | bytes accessed | tf_op | source)
XLA Modules:
  0.0 66.8 jit_solution(10711821877071600062)
XLA Ops:
  0.6 64.8 %train_step.1 = (f32[2,3,2,128,384]{4,3,2,1,0:T(8,128)S(1)}, f32[8,128]{1,0:T(8,128)S(1)}) custom-call(f32[128,256]{1,0:T(8,128)} %refs_0_.1, f32[128,256]{1,0:T(8,128)} %refs_1_.1, f32[1,128]{1,0:T(1,128)} %bitcast.3, s32[1,128]{1,0:T(1,128)} %bitcast.4, f32[256,384]{1,0:T(8,128)} %refs_4_.1, f32[384,384]{1,0:T(8,128)} %refs_5_.1, f32[384,128]{1,0:T(8,128)} %refs_6_.1, ...), custom_call_target="tpu_custom_call" | custom-call | tf_op jit(solution)/shard_map/train_step/pallas_call | solution.py:678
  65.4 1.4 %finish.1 = (f32[1,1]{1,0:T(1,128)}, f32[256,384]{1,0:T(8,128)}, f32[384,384]{1,0:T(8,128)}, f32[384,128]{1,0:T(8,128)}, f32[256,384]{1,0:T(8,128)}, /*index=5*/f32[384,384]{1,0:T(8,128)}, f32[384,128]{1,0:T(8,128)}) custom-call(f32[2,3,2,128,384]{4,3,2,1,0:T(8,128)S(1)} %get-tuple-element.16.res_ref, f32[8,128]{1,0:T(8,128)S(1)} %get-tuple-element.17.loss_in), custom_call_target="tpu_custom_call" | custom-call | tf_op jit(solution)/shard_map/finish/pallas_call | solution.py:688

commit v5 on v4

--- a/solution.py
+++ b/solution.py
@@ -22,7 +22,7 @@
 C00 = (((0,), (0,)), ((), ()))
 C11 = (((1,), (1,)), ((), ()))
 C10 = (((1,), (0,)), ((), ()))
-N_REMOTE = 192
+N_REMOTE = 208
 
 
 def mm(a, b, dims=C10):
@@ -88,6 +88,8 @@
         stats=vm(F32, nk, nx, 2 * n_small, ROWS),
         stat_all=vm(F32, 2 * n_small, ROWS),
         plane_t=vm(BF16, EMB, n_wide),
+        user_t=vm(BF16, EMB, n_wide),
+        item_tile=vm(BF16, 256, n_wide),
         grad_tile=vm(BF16, n_wide, 256),
         scores=vm(F32, n_small // 2, 256, n_wide),
         chunk_max=vm(F32, n_small // 2, 1, n_wide),
@@ -265,18 +267,22 @@
     s.meta_plane[z, y] = meta
     s.meta_small[k, x] = meta
     pl.semaphore_wait(barrier, len(greet))
-    meta_y = share(AY, s.meta_plane.at[z, y])
-    meta_x = share(AX, s.meta_small.at[k, x])
     v_first = plane_first(1)
+    meta_own = s.meta_plane.at[z, y, pl.ds(0, 3)]
+    meta_wide = plane_group().send(lambda r, d: meta_own, lambda r, d: meta_own)
+    meta_mine = s.meta_small.at[k, x, pl.ds(0, 3)]
+    meta_near = small_group().send(lambda r, d: meta_mine, lambda r, d: meta_mine)
     v_small = share(AX, s.small[1].at[k, x])
     forward(0)
     u_small = share(AX, s.small[0].at[k, x])
     u_first = plane_first(0)
-    meta_y.recv()
-    meta_z = share(AZ, s.meta_plane.at[z])
-    meta_x.recv()
-    meta_k = share(AK, s.meta_small.at[k])
     v_second = plane_second(1, v_first)
+    u_small.recv()
+    u_small_k = share(AK, s.small[0].at[k])
+    u_second = plane_second(0, u_first)
+    v_small.recv()
+    v_small_k = share(AK, s.small[1].at[k])
+
     def columns(ref, lq_out, id_out, id_row, count, nested):
         flat = ref[...].reshape(count * 8, ROWS)
         if count * 8 < ROWS:
@@ -291,19 +297,13 @@
             row_lo = flat[8 * i + 2:8 * i + 3].astype(jnp.int32)
             id_row[:, i * ROWS:(i + 1) * ROWS] = row_hi * 65536 + row_lo
 
-    meta_k.recv()
+    meta_near.recv()
     columns(s.meta_small, s.lqc_small, s.idc_small, s.idr_small, n_small, 0)
-    meta_z.recv()
+    meta_wide.recv()
     columns(s.meta_plane, s.lqc_plane, s.idc_plane, s.idr_plane, n_plane, ny)
 
     def transposed(value):
         return value.astype(F32).T.astype(BF16)
-
-    u_small.recv()
-    u_small_k = share(AK, s.small[0].at[k])
-    u_second = plane_second(0, u_first)
-    v_small.recv()
-    v_small_k = share(AK, s.small[1].at[k])
 
     for t in (0, 1):
         s.xt[t, k] = s.xf[t][...].T.astype(BF16)
@@ -399,6 +399,10 @@
             s.chunk_max[chunk, :, lanes] = peak
         return carry
 
+    for iz in range(nz):
+        for iy in range(ny):
+            i = iz * ny + iy
+            s.user_t[:, i * ROWS:(i + 1) * ROWS] = transposed(s.plane[0][iz, iy])
     lax.fori_loop(0, 3 * n_chunk // 4, wide_tile, 0)
 
     stats.recv()
@@ -474,14 +478,13 @@
 
     def item_chunk(stage, side, own):
         chunk = 2 * stage + own
-        grads = []
         for n in range(n_wide_tile):
             lanes = slice(n * 256, (n + 1) * 256)
             factor = jnp.exp(s.chunk_max[chunk, :, lanes] - s.row_max[:, lanes]) * s.row_inv[:, lanes]
-            grads.append((s.scores[chunk, :, lanes] * factor).astype(BF16))
-        total = mm(jnp.concatenate(grads, axis=1), s.plane[0][...].reshape(n_wide, EMB))
+            s.item_tile[:, lanes] = (s.scores[chunk, :, lanes] * factor).astype(BF16)
+        total = mm(s.user_t[...], s.item_tile[...], C11)
         for i, r in enumerate(stages[stage]):
-            s.parts[1][side * nx + wrap(AX, r)] = total[i * ROWS:(i + 1) * ROWS]
+            s.parts[1][side * nx + wrap(AX, r)] = total[:, i * ROWS:(i + 1) * ROWS]
 
     dv_core = Exchange([(i, None, at_peer(AK, 1)) for i in range(nx)])
     dv_x = along(AX)
@@ -492,7 +495,7 @@
             dv_core.post(2 * stage + i, s.parts[1].at[(1 - k) * nx + spot], s.from_core[1].at[spot])
         item_chunk(stage, k, 1)
         if 0 in turns:
-            s.parts[1][own_block] = s.parts[1][own_block] + mm(s.own_diag[...], u_own)
+            s.parts[1][own_block] = s.parts[1][own_block] + mm(u_own, s.own_diag[...], C00)
         for i, r in enumerate(turns):
             spot = wrap(AX, r)
             dv_core.copies[2 * stage + i].wait_recv()
@@ -578,7 +581,7 @@
     saved.recv()
     weight_grads(0)
     drain(middle)
-    grad_item = summed(1, dv_x)
+    grad_item = summed(1, dv_x).T
     backward(1, grad_item)
     hand_grads(1)
     weight_grads(1)

time: 67 us -> 66.8 us (level)
  no operation moved by 1% of the time
where the time goes in v5:
time: 66.8 us; the launch traced here: 66.7 us
  Pallas kernels  66.1 us (99%)
    pallas_call x1, Pallas kernels, device_step(): pl.pallas_call(functools.partial(step_kernel, grid, tree), out_shape=(jax...  64.7 us
    pallas_call x1, Pallas kernels, device_step(): pl.pallas_call(functools.partial(finish_kernel, float(devices * ROWS)), o...  1.42 us

profile of v5, /device:TPU:1, one launch (start us, length us, event | category | flops | bytes accessed | tf_op | source)
XLA Modules:
  0.0 66.7 jit_solution(15922074050079948620)
XLA Ops:
  0.6 64.7 %train_step.1 = (f32[2,3,2,128,384]{4,3,2,1,0:T(8,128)S(1)}, f32[8,128]{1,0:T(8,128)S(1)}) custom-call(f32[128,256]{1,0:T(8,128)} %refs_0_.1, f32[128,256]{1,0:T(8,128)} %refs_1_.1, f32[1,128]{1,0:T(1,128)} %bitcast.3, s32[1,128]{1,0:T(1,128)} %bitcast.4, f32[256,384]{1,0:T(8,128)} %refs_4_.1, f32[384,384]{1,0:T(8,128)} %refs_5_.1, f32[384,128]{1,0:T(8,128)} %refs_6_.1, ...), custom_call_target="tpu_custom_call" | custom-call | tf_op jit(solution)/shard_map/train_step/pallas_call | solution.py:681
  65.3 1.4 %finish.1 = (f32[1,1]{1,0:T(1,128)}, f32[256,384]{1,0:T(8,128)}, f32[384,384]{1,0:T(8,128)}, f32[384,128]{1,0:T(8,128)}, f32[256,384]{1,0:T(8,128)}, /*index=5*/f32[384,384]{1,0:T(8,128)}, f32[384,128]{1,0:T(8,128)}) custom-call(f32[2,3,2,128,384]{4,3,2,1,0:T(8,128)S(1)} %get-tuple-element.16.res_ref, f32[8,128]{1,0:T(8,128)S(1)} %get-tuple-element.17.loss_in), custom_call_target="tpu_custom_call" | custom-call | tf_op jit(solution)/shard_map/finish/pallas_call | solution.py:691
